TPU v7x, 64 devices: a 2x2x8 block of a 4x4x8 slice. The times are simulated.
64 devices in a mesh: dp: 4 (over x, y), cp: 16 (over z, core).
Axes of the slice: x: 2, y: 2, z: 8, core: 2. Of those that a mesh axis runs over, the one named last changes fastest.
The devices are a block of a 4x4x8 slice.
Arguments:
- x_tokens: bfloat16 [32, 8192, 640], P('dp', 'cp'), parts along dimension 0
- dy_tokens: bfloat16 [32, 8192, 640], P('dp', 'cp'), parts along dimension 0
- positions: int32 [32, 8192], P('dp', 'cp'), parts along dimension 0
- w_query: bfloat16 [640, 1024], replicated
- w_key: bfloat16 [640, 256], replicated
- w_value: bfloat16 [640, 256], replicated
- w_out: bfloat16 [1024, 640], replicated
- w_gate: bfloat16 [640, 2048], replicated
- w_up: bfloat16 [640, 2048], replicated
- w_down: bfloat16 [2048, 640], replicated
- g_attn_in: bfloat16 [640], replicated
- g_attn_out: bfloat16 [640], replicated
- g_mlp_in: bfloat16 [640], replicated
- g_mlp_out: bfloat16 [640], replicated
- g_query: bfloat16 [256], replicated
- g_key: bfloat16 [256], replicated
Outputs:
- output 1: bfloat16 [32, 8192, 640], P('dp', 'cp'), parts along dimension 0
- output 2: bfloat16 [32, 8192, 640], P('dp', 'cp'), parts along dimension 0
- output 3: bfloat16 [2560, 1024], P('dp'), parts along dimension 0
- output 4: bfloat16 [2560, 256], P('dp'), parts along dimension 0
- output 5: bfloat16 [2560, 256], P('dp'), parts along dimension 0
- output 6: bfloat16 [4096, 640], P('dp'), parts along dimension 0
- output 7: bfloat16 [2560, 2048], P('dp'), parts along dimension 0
- output 8: bfloat16 [2560, 2048], P('dp'), parts along dimension 0
- output 9: bfloat16 [8192, 640], P('dp'), parts along dimension 0
- output 10: bfloat16 [2560], P('dp'), parts along dimension 0
- output 11: bfloat16 [2560], P('dp'), parts along dimension 0
- output 12: bfloat16 [2560], P('dp'), parts along dimension 0
- output 13: bfloat16 [2560], P('dp'), parts along dimension 0
- output 14: bfloat16 [1024], P('dp'), parts along dimension 0
- output 15: bfloat16 [1024], P('dp'), parts along dimension 0
There are 4 independent parts. A program takes and returns all parts, laid end to end along the dimension named above; an argument that names none is the same for every part.
All inputs are finite; a program needn't handle non-finite values.
Results may differ from a plain program's by a relative error of at most 0.02.
Values are sent between devices in bfloat16 or wider.
A program may use at most 768 MiB of HBM per device.

v0:
```python
import functools
import jax
import jax.numpy as jnp
from jax import lax
from jax.sharding import PartitionSpec as P

NORM_EPS = 1e-6
ROPE_BASE = 10000.0


def window_size(model_dim):
    return 512 * min(2, 1 + model_dim // 2048)


def score_scale(model_dim, num_heads, head_dim):
    scalar = 256 if head_dim == 256 else model_dim // num_heads
    return scalar ** -0.5


def rms_scale(values, gain_vec):
    mean_sq = jnp.mean(values * values, axis=-1, keepdims=True)
    return values * lax.rsqrt(mean_sq + NORM_EPS) * (1.0 + gain_vec.astype(jnp.float32))


def rope_tables(pos_ids, head_dim):
    half_dim = head_dim // 2
    inv_freq = ROPE_BASE ** (-2.0 * jnp.arange(half_dim, dtype=jnp.float32) / head_dim)
    angles = pos_ids.astype(jnp.float32)[..., None] * inv_freq
    return jnp.cos(angles), jnp.sin(angles)


def head_prep(proj_vals, gain_vec, cos_tab, sin_tab):
    normed = rms_scale(proj_vals, gain_vec)
    half_dim = normed.shape[-1] // 2
    first_half = normed[..., :half_dim]
    second_half = normed[..., half_dim:]
    cos_part = cos_tab[..., None, :]
    sin_part = sin_tab[..., None, :]
    return jnp.concatenate([first_half * cos_part - second_half * sin_part, second_half * cos_part + first_half * sin_part], axis=-1)


def gelu_gate(gate_proj, up_proj):
    return jax.nn.gelu(gate_proj, approximate=True) * up_proj


def window_view(ext_vals, window):
    blocked = ext_vals.reshape((ext_vals.shape[0], ext_vals.shape[1] // window, window) + ext_vals.shape[2:])
    return jnp.concatenate([blocked[:, :-1], blocked[:, 1:]], axis=2)


def window_fold(win_grad, window):
    lead_part = win_grad[:, :, :window].astype(jnp.float32)
    trail_part = win_grad[:, :, window:].astype(jnp.float32)
    zero_block = jnp.zeros_like(lead_part[:, :1])
    fold_sum = jnp.concatenate([lead_part, zero_block], axis=1) + jnp.concatenate([zero_block, trail_part], axis=1)
    return fold_sum.reshape((fold_sum.shape[0], fold_sum.shape[1] * window) + fold_sum.shape[3:])


def make_attend(visible, score_mult, kv_heads, groups):
    def attend(q_rot, k_win, v_win):
        n_batch, blocks, window = visible.shape[0], visible.shape[1], visible.shape[2]
        head_dim = q_rot.shape[-1]
        q_blk = q_rot.reshape(n_batch, blocks, window, kv_heads, groups, head_dim)
        scores = jnp.einsum("bnqkgd,bnskd->bnkgqs", q_blk, k_win, preferred_element_type=jnp.float32) * score_mult
        scores = jnp.where(visible[:, :, None, None], scores, -1e30)
        prob_vals = jax.nn.softmax(scores, axis=-1).astype(jnp.bfloat16)
        attn_vals = jnp.einsum("bnkgqs,bnskd->bnqkgd", prob_vals, v_win, preferred_element_type=jnp.float32)
        return attn_vals.reshape(n_batch, blocks * window, kv_heads * groups * head_dim)
    return attend


def solution(mesh):
    cp_size = mesh.shape["cp"]
    to_next = [(idx, idx + 1) for idx in range(cp_size - 1)]
    to_prev = [(idx + 1, idx) for idx in range(cp_size - 1)]

    def local_step(x_tokens, dy_tokens, positions, w_query, w_key, w_value, w_out, w_gate, w_up, w_down, g_attn_in, g_attn_out, g_mlp_in, g_mlp_out, g_query, g_key):
        n_batch, tokens, model_dim = x_tokens.shape
        head_dim = g_query.shape[0]
        num_heads = w_query.shape[1] // head_dim
        kv_heads = w_key.shape[1] // head_dim
        window = window_size(model_dim)
        blocks = tokens // window
        tail_len = window - 1
        keep_len = tokens - tail_len
        shard_idx = lax.axis_index("cp")

        x_f32 = x_tokens.astype(jnp.float32)
        h_attn32, attn_in_back = jax.vjp(rms_scale, x_f32, g_attn_in.astype(jnp.float32))
        h_attn = h_attn32.astype(jnp.bfloat16)
        cos_tab, sin_tab = rope_tables(positions, head_dim)
        prep_fn = functools.partial(head_prep, cos_tab=cos_tab, sin_tab=sin_tab)
        q_proj = jnp.dot(h_attn, w_query, preferred_element_type=jnp.float32).reshape(n_batch, tokens, num_heads, head_dim)
        k_proj = jnp.dot(h_attn, w_key, preferred_element_type=jnp.float32).reshape(n_batch, tokens, kv_heads, head_dim)
        q_rot32, q_back = jax.vjp(prep_fn, q_proj, g_query.astype(jnp.float32))
        k_rot32, k_back = jax.vjp(prep_fn, k_proj, g_key.astype(jnp.float32))
        q_rot = q_rot32.astype(jnp.bfloat16)
        k_rot = k_rot32.astype(jnp.bfloat16)
        v_val = jnp.dot(h_attn, w_value, preferred_element_type=jnp.float32).astype(jnp.bfloat16).reshape(n_batch, tokens, kv_heads, head_dim)

        k_prev, v_prev, pos_prev = lax.ppermute((k_rot[:, keep_len:], v_val[:, keep_len:], positions[:, keep_len:]), "cp", to_next)
        kv_pad = jnp.zeros((n_batch, 1, kv_heads, head_dim), jnp.bfloat16)
        k_win = window_view(jnp.concatenate([kv_pad, k_prev, k_rot], axis=1), window)
        v_win = window_view(jnp.concatenate([kv_pad, v_prev, v_val], axis=1), window)
        pos_win = window_view(jnp.concatenate([jnp.zeros((n_batch, 1), jnp.int32), pos_prev, positions], axis=1), window)
        ext_index = jnp.arange(blocks)[:, None] * window + jnp.arange(2 * window)[None, :]
        valid = (ext_index >= window) | ((ext_index >= 1) & (shard_idx > 0))
        q_pos = positions.reshape(n_batch, blocks, window)[..., None]
        visible = valid[None, :, None, :] & (pos_win[:, :, None, :] > q_pos - window) & (pos_win[:, :, None, :] <= q_pos)
        attend = make_attend(visible, score_scale(model_dim, num_heads, head_dim), kv_heads, num_heads // kv_heads)
        attn32, attn_back = jax.vjp(attend, q_rot, k_win, v_win)
        attn_out = attn32.astype(jnp.bfloat16)

        o_proj = jnp.dot(attn_out, w_out, preferred_element_type=jnp.float32)
        post_attn32, post_attn_back = jax.vjp(rms_scale, o_proj, g_attn_out.astype(jnp.float32))
        x_mid32 = (x_f32 + post_attn32).astype(jnp.bfloat16).astype(jnp.float32)
        h_mlp32, mlp_in_back = jax.vjp(rms_scale, x_mid32, g_mlp_in.astype(jnp.float32))
        h_mlp = h_mlp32.astype(jnp.bfloat16)
        gate_proj = jnp.dot(h_mlp, w_gate, preferred_element_type=jnp.float32)
        up_proj = jnp.dot(h_mlp, w_up, preferred_element_type=jnp.float32)
        gated32, gated_back = jax.vjp(gelu_gate, gate_proj, up_proj)
        hidden_act = gated32.astype(jnp.bfloat16)
        down_proj = jnp.dot(hidden_act, w_down, preferred_element_type=jnp.float32)
        post_mlp32, post_mlp_back = jax.vjp(rms_scale, down_proj, g_mlp_out.astype(jnp.float32))
        y_tokens = (x_mid32 + post_mlp32).astype(jnp.bfloat16)

        dy32 = dy_tokens.astype(jnp.float32)
        d_down32, dg_mlp_out = post_mlp_back(dy32)
        d_down = d_down32.astype(jnp.bfloat16)
        dw_down = jnp.einsum("btf,btd->fd", hidden_act, d_down, preferred_element_type=jnp.float32)
        d_hidden = jnp.einsum("btd,fd->btf", d_down, w_down, preferred_element_type=jnp.float32).astype(jnp.bfloat16)
        d_gate32, d_up32 = gated_back(d_hidden.astype(jnp.float32))
        d_gate = d_gate32.astype(jnp.bfloat16)
        d_up = d_up32.astype(jnp.bfloat16)
        dw_gate = jnp.einsum("btd,btf->df", h_mlp, d_gate, preferred_element_type=jnp.float32)
        dw_up = jnp.einsum("btd,btf->df", h_mlp, d_up, preferred_element_type=jnp.float32)
        d_hmlp = jnp.einsum("btf,df->btd", d_gate, w_gate, preferred_element_type=jnp.float32) + jnp.einsum("btf,df->btd", d_up, w_up, preferred_element_type=jnp.float32)
        d_mid_part, dg_mlp_in = mlp_in_back(d_hmlp)
        d_mid = dy32 + d_mid_part
        d_oproj32, dg_attn_out = post_attn_back(d_mid)
        d_oproj = d_oproj32.astype(jnp.bfloat16)
        dw_out = jnp.einsum("bte,btd->ed", attn_out, d_oproj, preferred_element_type=jnp.float32)
        d_attn = jnp.einsum("btd,ed->bte", d_oproj, w_out, preferred_element_type=jnp.float32).astype(jnp.bfloat16)
        dq_rot, dk_win, dv_win = attn_back(d_attn.astype(jnp.float32))

        dk_ext = window_fold(dk_win, window)
        dv_ext = window_fold(dv_win, window)
        dk_next, dv_next = lax.ppermute((dk_ext[:, 1:window].astype(jnp.bfloat16), dv_ext[:, 1:window].astype(jnp.bfloat16)), "cp", to_prev)
        dk_total = jnp.concatenate([dk_ext[:, window:window + keep_len], dk_ext[:, window + keep_len:] + dk_next.astype(jnp.float32)], axis=1)
        dv_total = jnp.concatenate([dv_ext[:, window:window + keep_len], dv_ext[:, window + keep_len:] + dv_next.astype(jnp.float32)], axis=1)
        dq_proj, dg_query = q_back(dq_rot.astype(jnp.float32))
        dk_proj, dg_key = k_back(dk_total)
        dq_flat = dq_proj.astype(jnp.bfloat16).reshape(n_batch, tokens, num_heads * head_dim)
        dk_flat = dk_proj.astype(jnp.bfloat16).reshape(n_batch, tokens, kv_heads * head_dim)
        dv_flat = dv_total.astype(jnp.bfloat16).reshape(n_batch, tokens, kv_heads * head_dim)
        dw_query = jnp.einsum("btd,bte->de", h_attn, dq_flat, preferred_element_type=jnp.float32)
        dw_key = jnp.einsum("btd,bte->de", h_attn, dk_flat, preferred_element_type=jnp.float32)
        dw_value = jnp.einsum("btd,bte->de", h_attn, dv_flat, preferred_element_type=jnp.float32)
        d_hattn = (jnp.einsum("bte,de->btd", dq_flat, w_query, preferred_element_type=jnp.float32)
                   + jnp.einsum("bte,de->btd", dk_flat, w_key, preferred_element_type=jnp.float32)
                   + jnp.einsum("bte,de->btd", dv_flat, w_value, preferred_element_type=jnp.float32))
        dx_part, dg_attn_in = attn_in_back(d_hattn)
        dx_tokens = (d_mid + dx_part).astype(jnp.bfloat16)
        grads = lax.psum((dw_query, dw_key, dw_value, dw_out, dw_gate, dw_up, dw_down, dg_attn_in, dg_attn_out, dg_mlp_in, dg_mlp_out, dg_query, dg_key), "cp")
        return (y_tokens, dx_tokens) + tuple(item.astype(jnp.bfloat16) for item in grads)

    seq_spec = P("dp", "cp", None)
    in_specs = (seq_spec, seq_spec, P("dp", "cp")) + (P(None, None),) * 7 + (P(None),) * 6
    out_specs = (seq_spec, seq_spec) + (P("dp", None),) * 7 + (P("dp"),) * 6
    return jax.shard_map(local_step, mesh=mesh, in_specs=in_specs, out_specs=out_specs, check_vma=False)
```

profile of v0, /device:TPU:30, one launch (start us, length us, event | category | flops | bytes accessed | tf_op | source)
XLA Modules:
  0.0 1178.5 jit_solution(797419984946161481)
XLA Ops:
  54.8 13.0 %fusion.104 = f32[8,512,1024]{2,1,0:T(8,128)} fusion(bf16[640,1024]{1,0:T(8,128)(2,1)} %param.19, bf16[8,512,640]{2,1,0:T(8,128)(2,1)} %param.16, f32[640]{0:T(1024)S(1)} %convert_add_fusion.8, f32[8,512]{1,0:T(8,128)S(1)} %fusion.115), kind=kOutput, calls=%fused_computation.173 | convolution fusion | flops 5379194880 | bytes 23349760 | tf_op jit(solution)/shard_map/dot_general | solution.py:93
  67.8 20.4 %reshape.389 = f32[8,512,4,256]{3,2,1,0:T(4,128)} reshape(f32[8,512,1024]{2,1,0:T(8,128)} %fusion.104) | data formatting | bytes 33554432 | tf_op jit(solution)/shard_map/reshape | solution.py:93
  88.1 11.4 multiply_reduce_fusion.1
  166.7 10.5 copy.253
  177.1 10.4 copy.252
  187.6 29.4 %fusion.9 = (f32[8,4,512]{2,1,0:T(4,128)S(1)}, f32[8,1024,512,4]{2,1,3,0:T(8,128)}) fusion(pred[8,512,1024]{1,2,0:T(8,128)(4,1)} %compare_and_fusion, bf16[8,512,4,128]{3,1,2,0:T(8,128)(2,1)} %get-tuple-element.48, bf16[8,512,4,128]{3,1,2,0:T(8,128)(2,1)} %get-tuple-element.47, bf16[8,1,512,1,256]{4,2,0,3,1:T(8,128)(2,1)} %copy.253, ...), kind=kOutput, calls=%fused_computation.14 | convolution fusion | flops 8665415680 | bytes 83951616 | tf_op jit(solution)/shard_map/jvp(bnqkgd,bnskd->bnkgqs)/dot_general | solution.py:64
  217.0 22.5 %fusion.133 = f32[8,4,512]{2,1,0:T(4,128)S(1)} fusion(f32[8,4,512]{2,1,0:T(4,128)S(1)} %get-tuple-element.71, f32[8,1024,512,4]{2,1,3,0:T(8,128)} %get-tuple-element.72, pred[8,512,1024]{1,2,0:T(8,128)(4,1)} %compare_and_fusion), kind=kLoop, calls=%fused_computation.230 | loop fusion | flops 67092480 | bytes 71434240 | tf_op jit(solution)/shard_map/jvp()/reduce_sum | solution.py:66
  240.2 32.4 %fusion.51 = bf16[8,256,4,512]{3,1,2,0:T(8,128)(2,1)} fusion(bf16[8,1,512,1,256]{2,4,0,3,1:T(8,128)(2,1)} %copy.251, bf16[8,1,512,1,256]{2,4,0,3,1:T(8,128)(2,1)} %copy.250, f32[8,4,512]{2,1,0:T(4,128)S(1)} %fusion.133, f32[8,4,512]{2,1,0:T(4,128)S(1)} %get-tuple-element.71, f32[8,1024,512,4]{2,1,3,0:T(8,128)} %get-tuple-element.72, ...), kind=kOutput, calls=%fused_computation.102 | convolution fusion | flops 8686403584 | bytes 84017152 | tf_op jit(solution)/shard_map/jvp(bnkgqs,bnskd->bnqkgd)/dot_general | solution.py:67
  289.1 19.2 %fusion.83 = f32[8,512,2048]{2,1,0:T(8,128)} fusion(bf16[640,2048]{1,0:T(8,128)(2,1)} %param.23, bf16[8,512,640]{2,1,0:T(8,128)(2,1)S(1)} %get-tuple-element.42, f32[640]{0:T(1024)S(1)} %copy-done.58, f32[8,512]{1,0:T(8,128)S(1)} %fusion.118), kind=kOutput, calls=%fused_computation.150 | convolution fusion | flops 10747904000 | bytes 41437696 | tf_op jit(solution)/shard_map/dot_general | solution.py:119
  308.3 33.2 %multiply_convert_fusion = (bf16[8,512,2048]{2,1,0:T(8,128)(2,1)}, f32[8,512,2048]{2,1,0:T(8,128)}) fusion(f32[8,512,2048]{2,1,0:T(8,128)} %fusion.83, bf16[640,2048]{1,0:T(8,128)(2,1)S(1)} %copy-done, bf16[8,512,640]{2,1,0:T(8,128)(2,1)} %copy-done.5, f32[640]{0:T(1024)S(1)} %copy-done.58, f32[8,512]{1,0:T(8,128)S(1)} %fusion.118), kind=kOutput, calls=%fused_computation.31 | convolution fusion | flops 10831790080 | bytes 91769344 | tf_op jit(solution)/shard_map/dot_general | solution.py:120
  341.5 16.7 %multiply_reduce_fusion.4 = (f32[8,512]{1,0:T(8,128)S(1)}, f32[8,512,640]{2,1,0:T(8,128)S(1)}) fusion(bf16[8,512,2048]{2,1,0:T(8,128)(2,1)} %get-tuple-element.75, bf16[2048,640]{1,0:T(8,128)(2,1)S(1)} %copy-done.70), kind=kOutput, calls=%fused_computation.90 | convolution fusion | flops 10742657024 | bytes 29900800 | tf_op jit(solution)/shard_map/dot_general | solution.py:123
  371.8 44.6 %fusion.10 = (bf16[8,512,2048]{2,1,0:T(8,128)(2,1)}, bf16[8,512,2048]{2,1,0:T(8,128)(2,1)}) fusion(f32[8,512,2048]{2,1,0:T(8,128)} %fusion.83, f32[8,512,2048]{2,1,0:T(8,128)} %get-tuple-element.76, bf16[8,512,640]{2,1,0:T(8,128)(2,1)} %get-tuple-element.49, bf16[2048,640]{1,0:T(8,128)(2,1)} %param.25), kind=kOutput, calls=%fused_computation.19 | convolution fusion | flops 10955522048 | bytes 108527616 | tf_op jit(solution)/shard_map/btd,fd->btf/dot_general | solution.py:131
  416.5 19.3 %fusion.81 = f32[8,512,640]{2,1,0:T(8,128)} fusion(bf16[8,512,2048]{2,1,0:T(8,128)(2,1)} %get-tuple-element.44, bf16[640,2048]{1,0:T(8,128)(2,1)} %param.23), kind=kOutput, calls=%fused_computation.148 | convolution fusion | flops 10737418240 | bytes 29884416 | tf_op jit(solution)/shard_map/btf,df->btd/dot_general | solution.py:137
  435.8 23.6 %fusion.36 = (f32[640]{0:T(1024)}, f32[8,512]{1,0:T(8,128)S(1)}, f32[8,512,640]{2,1,0:T(8,128)}) fusion(bf16[8,512,640]{2,1,0:T(8,128)(2,1)} %copy-done.5, f32[8,512]{1,0:T(8,128)S(1)} %fusion.118, f32[640]{0:T(1024)S(1)} %copy-done.58, f32[8,512,640]{2,1,0:T(8,128)} %fusion.81, bf16[8,512,2048]{2,1,0:T(8,128)(2,1)} %get-tuple-element.43, ...), kind=kOutput, calls=%fused_computation.72 | convolution fusion | flops 10758384640 | bytes 45650944 | tf_op jit(solution)/shard_map/btf,df->btd/dot_general | solution.py:137
  459.5 12.6 %multiply_reduce_fusion.2 = (f32[640]{0:T(1024)}, f32[8,512]{1,0:T(8,128)S(1)}, f32[8,512,640]{2,1,0:T(8,128)S(1)}) fusion(f32[8,512,640]{2,1,0:T(8,128)} %copy-done.3, f32[8,512]{1,0:T(8,128)S(1)} %copy-done.33, f32[640]{0:T(1024)S(1)} %copy-done.52, f32[8,512]{1,0:T(8,128)S(1)} %multiply_multiply_fusion.6, bf16[8,512,640]{2,1,0:T(8,128)(2,1)} %copy-done.5, ...), kind=kLoop, calls=%fused_computation.87 | loop fusion | flops 36695424 | bytes 42016256 | tf_op jit(solution)/shard_map/transpose(jvp())/reduce_sum | solution.py:22
  493.4 11.4 copy.245
  504.9 31.8 %fusion.59 = bf16[8,1,1024,1,256]{2,4,0,3,1:T(8,128)(2,1)} fusion(bf16[8,256,4,512]{3,1,2,0:T(8,128)(2,1)} %bitcast.303, f32[8,4,512]{2,1,0:T(4,128)S(1)} %copy-done.35, f32[8,4,512]{2,1,0:T(4,128)S(1)} %copy-done.50, f32[8,1024,512,4]{2,1,3,0:T(8,128)} %get-tuple-element.72, pred[8,512,1024]{1,2,0:T(8,128)(4,1)} %compare_and_fusion), kind=kOutput, calls=%fused_computation.108 | convolution fusion | flops 8675917824 | bytes 84017152 | tf_op jit(solution)/shard_map/transpose(jvp(bnkgqs,bnskd->bnqkgd))/dot_general | solution.py:67
  536.7 46.5 %fusion.8 = (f32[8,4,512]{2,1,0:T(4,128)S(1)}, bf16[8,4,512,1024]{2,3,1,0:T(8,128)(2,1)}) fusion(f32[8,4,512]{2,1,0:T(4,128)S(1)} %copy-done.48, f32[8,4,512]{2,1,0:T(4,128)S(1)} %copy-done.50, f32[8,1024,512,4]{2,1,3,0:T(8,128)} %get-tuple-element.72, pred[8,512,1024]{1,2,0:T(8,128)(4,1)} %compare_and_fusion, bf16[8,256,4,512]{3,1,2,0:T(8,128)(2,1)} %bitcast.304, ...), kind=kOutput, calls=%fused_computation.10 | convolution fusion | flops 8732524544 | bytes 117637120 | tf_op jit(solution)/shard_map/transpose(jvp(bnkgqs,bnskd->bnqkgd))/dot_general | solution.py:67
  583.3 46.8 %convert_convert_fusion = f32[8,512,4,256]{3,1,2,0:T(8,128)} fusion(bf16[8,4,512,1024]{2,3,1,0:T(8,128)(2,1)} %get-tuple-element.81, f32[8,4,512]{2,1,0:T(4,128)S(1)} %neg.13, f32[8,4,512]{2,1,0:T(4,128)S(1)} %copy-done.35, pred[8,512,1024]{1,2,0:T(8,128)(4,1)} %compare_and_fusion, bf16[8,1,512,1,256]{4,2,0,3,1:T(8,128)(2,1)S(1)} %copy-done.19, ...), kind=kOutput, calls=%fused_computation.99 | convolution fusion | flops 8757706752 | bytes 126025728 | tf_op jit(solution)/shard_map/transpose(jvp(bnqkgd,bnskd->bnkgqs))/dot_general | solution.py:64
  630.1 42.8 %fusion.58 = bf16[8,1,1024,1,256]{4,2,0,3,1:T(8,128)(2,1)} fusion(bf16[8,512,4,128]{3,1,2,0:T(8,128)(2,1)} %get-tuple-element.48, bf16[8,512,4,128]{3,1,2,0:T(8,128)(2,1)} %get-tuple-element.47, bf16[8,4,512,1024]{2,3,1,0:T(8,128)(2,1)} %get-tuple-element.81, f32[8,4,512]{2,1,0:T(4,128)S(1)} %neg.13, f32[8,4,512]{2,1,0:T(4,128)S(1)} %copy-done.35, ...), kind=kOutput, calls=%fused_computation.107 | convolution fusion | flops 8759803904 | bytes 117637120 | tf_op jit(solution)/shard_map/transpose(jvp(bnqkgd,bnskd->bnkgqs))/dot_general | solution.py:64
  679.7 13.3 %copy.204 = f32[8,2,512,1,256]{2,1,4,0,3:T(2,128)} copy(f32[8,2,512,1,256]{4,2,0,3,1:T(8,128)} %convert_add_fusion.4) | data formatting | bytes 16777216 | tf_op jit(solution)/shard_map/add | solution.py:55
  693.0 12.2 %reshape.395 = f32[8,1024,1,256]{1,3,0,2:T(8,128)} reshape(f32[8,2,512,1,256]{2,1,4,0,3:T(2,128)} %copy.204) | data formatting | bytes 16777216 | tf_op jit(solution)/shard_map/reshape | solution.py:56
  709.9 11.8 %convolution_bitcast_fusion.3 = f32[1024,640]{1,0:T(8,128)} fusion(bf16[8,512,1024]{1,2,0:T(8,128)(2,1)} %bitcast.309, bf16[8,512,640]{2,1,0:T(8,128)(2,1)} %copy-done.17), kind=kOutput, calls=%fused_computation.165 | convolution fusion | flops 5368709120 | bytes 16252928 | tf_op jit(solution)/shard_map/bte,btd->ed/dot_general | solution.py:142
  721.7 17.2 %convolution_bitcast_fusion.2 = f32[640,2048]{1,0:T(8,128)} fusion(bf16[8,512,2048]{2,1,0:T(8,128)(2,1)} %get-tuple-element.44, bf16[8,512,640]{2,1,0:T(8,128)(2,1)S(1)} %bitcast.299, f32[640]{0:T(1024)S(1)} %copy-done.59, f32[8,512]{1,0:T(8,128)S(1)} %copy-done.43), kind=kOutput, calls=%fused_computation.128 | convolution fusion | flops 10747904000 | bytes 27281920 | tf_op jit(solution)/shard_map/btd,btf->df/dot_general | solution.py:135
  738.9 17.3 %convolution_bitcast_fusion.1 = f32[640,2048]{1,0:T(8,128)} fusion(bf16[8,512,2048]{2,1,0:T(8,128)(2,1)} %get-tuple-element.43, bf16[8,512,640]{2,1,0:T(8,128)(2,1)S(1)} %bitcast.299, f32[640]{0:T(1024)S(1)} %copy-done.59, f32[8,512]{1,0:T(8,128)S(1)} %copy-done.43), kind=kOutput, calls=%fused_computation.127 | convolution fusion | flops 10747904000 | bytes 27281920 | tf_op jit(solution)/shard_map/btd,btf->df/dot_general | solution.py:136
  756.2 17.3 %convolution_bitcast_fusion = f32[2048,640]{1,0:T(8,128)} fusion(bf16[8,512,2048]{2,1,0:T(8,128)(2,1)} %get-tuple-element.75, bf16[8,512,640]{2,1,0:T(8,128)(2,1)S(1)} %bitcast.306), kind=kOutput, calls=%fused_computation.126 | convolution fusion | flops 10737418240 | bytes 27262976 | tf_op jit(solution)/shard_map/btf,btd->fd/dot_general | solution.py:130
  805.9 11.5 multiply_reduce_fusion
  827.3 12.3 %copy.202 = bf16[8,512,4,256]{1,3,2,0:T(8,128)(2,1)} copy(bf16[8,512,4,256]{3,1,2,0:T(8,128)(2,1)} %fusion.26) | data formatting | bytes 16777216 | tf_op jit(solution)/shard_map/convert_element_type | solution.py:153
  844.0 12.9 %convolution_bitcast_fusion.4 = f32[640,1024]{1,0:T(8,128)} fusion(bf16[8,512,1024]{1,2,0:T(8,128)(2,1)} %bitcast.301, bf16[8,512,640]{2,1,0:T(8,128)(2,1)} %param.16, f32[640]{0:T(1024)S(1)} %copy-done.54, f32[8,512]{1,0:T(8,128)S(1)} %copy-done.37), kind=kOutput, calls=%fused_computation.166 | convolution fusion | flops 5379194880 | bytes 16271872 | tf_op jit(solution)/shard_map/btd,bte->de/dot_general | solution.py:156
  901.9 11.9 %fusion.38 = (f32[640]{0:T(1024)S(1)}, f32[8,512]{1,0:T(8,128)S(1)}, f32[8,512,640]{2,1,0:T(8,128)}) fusion(bf16[8,512,640]{2,1,0:T(8,128)(2,1)S(1)} %bitcast.290, f32[8,512]{1,0:T(8,128)S(1)} %copy-done.37, f32[640]{0:T(1024)S(1)} %copy-done.54, bf16[640,256]{1,0:T(8,128)(2,1)S(1)} %copy-done.24, bf16[8,511,256]{2,1,0:T(8,128)(2,1)S(1)} %fusion.92, ...), kind=kOutput, calls=%fused_computation.74 | convolution fusion | flops 1369959808 | bytes 39162880 | tf_op jit(solution)/shard_map/bte,de->btd/dot_general | solution.py:161
  913.9 10.9 fusion.44
  924.7 253.6 %all-reduce.10 = (bf16[640,1024]{1,0:T(8,128)(2,1)}, bf16[640,256]{1,0:T(8,128)(2,1)}, bf16[640,256]{1,0:T(8,128)(2,1)}, bf16[1024,640]{1,0:T(8,128)(2,1)}, bf16...) all-reduce(f32[640,1024]{1,0:T(8,128)} %convolution_bitcast_fusion., ...), channel_id=1, replica_groups=mesh['dp'=4,'cp'=16] {'cp'}, use_global_device_ids=true, to_apply=%region_15.16 | all-reduce | flops 5573632 | bytes 33441792 | tf_op jit(solution)/shard_map/psum | solution.py:164
  (288 shorter events, 275.5 us)
Async XLA Ops:
  0.6 307.6 %copy-start = (bf16[640,2048]{1,0:T(8,128)(2,1)S(1)}, bf16[640,2048]{1,0:T(8,128)(2,1)}, u32[]{:S(2)}) copy-start(bf16[640,2048]{1,0:T(8,128)(2,1)} %param.24) | copy-start | bytes 7864324
  1.5 53.2 %copy-start.53 = (f32[640]{0:T(1024)}, f32[640]{0:T(1024)S(1)}, u32[]{:S(2)}) copy-start(f32[640]{0:T(1024)S(1)} %convert_add_fusion.8) | copy-start | bytes 7684
  5.7 49.0 %copy-start.36 = (f32[8,512]{1,0:T(8,128)}, f32[8,512]{1,0:T(8,128)S(1)}, u32[]{:S(2)}) copy-start(f32[8,512]{1,0:T(8,128)S(1)} %fusion.115) | copy-start | bytes 49156
  13.3 110.2 %collective-permute-start = (bf16[8,511,1,256]{3,0,2,1:T(8,128)(2,1)}, bf16[8,511,1,256]{3,0,2,1:T(8,128)(2,1)}, u32[]{:S(2)}, u32[]{:S(2)}) collective-permute-start(bf16[8,511,1,256]{3,0,2,1:T(8,128)(2,1)} %copy.177), channel_id=1, source_target_pairs={{0,1},{1,2},{2,3},{3,4},{4,5},{5,6},{6,7},{7,8},{8,9},{9,10},{10,1... | collective-permute-start | bytes 6279176 | tf_op jit(solution)/shard_map/ppermute | solution.py:101
  16.6 100.9 %collective-permute-start.1 = (s32[8,511]{1,0:T(8,128)S(1)}, s32[8,511]{1,0:T(8,128)S(1)}, u32[]{:S(2)}, u32[]{:S(2)}) collective-permute-start(s32[8,511]{1,0:T(8,128)S(1)} %slice.75), channel_id=1, source_target_pairs={{0,1},{1,2},{2,3},{3,4},{4,5},{5,6},{6,7},{7,8},{8,9},{9,10},{10,1... | collective-permute-start | bytes 49064 | tf_op jit(solution)/shard_map/ppermute | solution.py:101
  19.6 26.3 %copy-start.27 = (f32[8,512]{1,0:T(8,128)}, f32[8,512]{1,0:T(8,128)S(1)}, u32[]{:S(2)}) copy-start(f32[8,512]{1,0:T(8,128)S(1)} %get-tuple-element.68) | copy-start | bytes 49156
  19.6 26.3 %copy-start.64 = (f32[128]{0:T(128)}, f32[128]{0:T(128)S(1)}, u32[]{:S(2)}) copy-start(f32[128]{0:T(128)S(1)} %multiply_power_fusion) | copy-start | bytes 1540
  23.0 15.0 %copy-start.44 = (f32[8,512]{1,0:T(8,128)}, f32[8,512]{1,0:T(8,128)S(1)}, u32[]{:S(2)}) copy-start(f32[8,512]{1,0:T(8,128)S(1)} %get-tuple-element.69) | copy-start | bytes 49156
  23.0 14.9 %copy-start.62 = (f32[256]{0:T(256)}, f32[256]{0:T(256)S(1)}, u32[]{:S(2)}) copy-start(f32[256]{0:T(256)S(1)} %convert_add_fusion.10) | copy-start | bytes 3076
  42.4 97.3 %collective-permute-start.2 = (bf16[8,511,1,256]{3,0,2,1:T(8,128)(2,1)}, bf16[8,511,1,256]{3,0,2,1:T(8,128)(2,1)}, u32[]{:S(2)}, u32[]{:S(2)}) collective-permute-start(bf16[8,511,1,256]{3,0,2,1:T(8,128)(2,1)} %copy.182), channel_id=1, source_target_pairs={{0,1},{1,2},{2,3},{3,4},{4,5},{5,6},{6,7},{7,8},{8,9},{9,10},{10,1... | collective-permute-start | bytes 6279176 | tf_op jit(solution)/shard_map/ppermute | solution.py:101
  67.7 35.9 %copy-start.60 = (f32[256]{0:T(256)}, f32[256]{0:T(256)S(1)}, u32[]{:S(2)}) copy-start(f32[256]{0:T(256)S(1)} %convert_add_fusion.9) | copy-start | bytes 3076
  88.1 14.3 %copy-start.67 = (bf16[640]{0:T(1024)(128)(2,1)S(1)}, bf16[640]{0:T(1024)(128)(2,1)}, u32[]{:S(2)}) copy-start(bf16[640]{0:T(1024)(128)(2,1)} %param.29) | copy-start | bytes 3844
  88.1 15.0 %copy-start.68 = (bf16[640]{0:T(1024)(128)(2,1)S(1)}, bf16[640]{0:T(1024)(128)(2,1)}, u32[]{:S(2)}) copy-start(bf16[640]{0:T(1024)(128)(2,1)} %param.28) | copy-start | bytes 3844
  88.1 15.0 %copy-start.69 = (bf16[640]{0:T(1024)(128)(2,1)S(1)}, bf16[640]{0:T(1024)(128)(2,1)}, u32[]{:S(2)}) copy-start(bf16[640]{0:T(1024)(128)(2,1)} %param.27) | copy-start | bytes 3844
  217.0 23.1 %copy-start.49 = (f32[8,4,512]{2,1,0:T(4,128)}, f32[8,4,512]{2,1,0:T(4,128)S(1)}, u32[]{:S(2)}) copy-start(f32[8,4,512]{2,1,0:T(4,128)S(1)} %get-tuple-element.71) | copy-start | bytes 196612
  239.5 33.0 %copy-start.34 = (f32[8,4,512]{2,1,0:T(4,128)}, f32[8,4,512]{2,1,0:T(4,128)S(1)}, u32[]{:S(2)}) copy-start(f32[8,4,512]{2,1,0:T(4,128)S(1)} %fusion.133) | copy-start | bytes 196612
  287.4 172.1 %copy-start.42 = (f32[8,512]{1,0:T(8,128)}, f32[8,512]{1,0:T(8,128)S(1)}, u32[]{:S(2)}) copy-start(f32[8,512]{1,0:T(8,128)S(1)} %fusion.118) | copy-start | bytes 49156
  308.3 33.2 %copy-start.70 = (bf16[2048,640]{1,0:T(8,128)(2,1)S(1)}, bf16[2048,640]{1,0:T(8,128)(2,1)}, u32[]{:S(2)}) copy-start(bf16[2048,640]{1,0:T(8,128)(2,1)} %param.25) | copy-start | bytes 7864324
  341.5 16.8 %copy-start.55 = (f32[640]{0:T(1024)S(1)}, f32[640]{0:T(1024)}, u32[]{:S(2)}) copy-start(f32[640]{0:T(1024)} %convert_add_fusion.5) | copy-start | bytes 7684
  435.8 23.7 %copy-start.41 = (f32[8,512]{1,0:T(8,128)S(1)}, f32[8,512]{1,0:T(8,128)}, u32[]{:S(2)}) copy-start(f32[8,512]{1,0:T(8,128)} %copy-done.40) | copy-start | bytes 49156
  435.8 23.7 %copy-start.33 = (f32[8,512]{1,0:T(8,128)S(1)}, f32[8,512]{1,0:T(8,128)}, u32[]{:S(2)}) copy-start(f32[8,512]{1,0:T(8,128)} %copy-done.32) | copy-start | bytes 49156
  435.8 23.7 %copy-start.52 = (f32[640]{0:T(1024)S(1)}, f32[640]{0:T(1024)}, u32[]{:S(2)}) copy-start(f32[640]{0:T(1024)} %get-tuple-element.84) | copy-start | bytes 7684
  504.9 31.8 %copy-start.48 = (f32[8,4,512]{2,1,0:T(4,128)S(1)}, f32[8,4,512]{2,1,0:T(4,128)}, u32[]{:S(2)}) copy-start(f32[8,4,512]{2,1,0:T(4,128)} %multiply_divide_fusion) | copy-start | bytes 196612
  536.7 46.6 %copy-start.19 = (bf16[8,1,512,1,256]{4,2,0,3,1:T(8,128)(2,1)S(1)}, bf16[8,1,512,1,256]{4,2,0,3,1:T(8,128)(2,1)}, u32[]{:S(2)}) copy-start(bf16[8,1,512,1,256]{4,2,0,3,1:T(8,128)(2,1)} %copy.253) | copy-start | bytes 6291460
  721.7 34.5 %slice-start.17 = ((s8[5242880]{0:T(1024)(128)(4,1)}), s8[4194304]{0:T(1024)(128)(4,1)S(1)}, s32[]{:S(2)}) async-start(s8[5242880]{0:T(1024)(128)(4,1)} %bitcast.305), calls=%async_computation.17 | async-start | bytes 8388608
  738.9 17.3 %slice-start.18 = ((s8[5242880]{0:T(1024)(128)(4,1)}), s8[1048576]{0:T(1024)(128)(4,1)S(1)}, s32[]{:S(2)}) async-start(s8[5242880]{0:T(1024)(128)(4,1)} %bitcast.305), calls=%async_computation.18 | async-start | bytes 2097152
  756.2 17.3 %copy-start.18 = (bf16[8,1,1024,1,256]{2,4,0,3,1:T(8,128)(2,1)S(1)}, bf16[8,1,1024,1,256]{2,4,0,3,1:T(8,128)(2,1)}, u32[]{:S(2)}) copy-start(bf16[8,1,1024,1,256]{2,4,0,3,1:T(8,128)(2,1)} %fusion.59) | copy-start | bytes 12582916
  794.6 101.7 %collective-permute-start.4 = (bf16[8,511,1,256]{3,0,2,1:T(8,128)(2,1)}, bf16[8,511,1,256]{3,0,2,1:T(8,128)(2,1)}, u32[]{:S(2)}, u32[]{:S(2)}) collective-permute-start(bf16[8,511,1,256]{3,0,2,1:T(8,128)(2,1)} %copy.210), channel_id=1, source_target_pairs={{1,0},{2,1},{3,2},{4,3},{5,4},{6,5},{7,6},{8,7},{9,8},{10,9},{11,1... | collective-permute-start | bytes 6279176 | tf_op jit(solution)/shard_map/ppermute | solution.py:148
  827.2 16.7 %copy-start.37 = (f32[8,512]{1,0:T(8,128)S(1)}, f32[8,512]{1,0:T(8,128)}, u32[]{:S(2)}) copy-start(f32[8,512]{1,0:T(8,128)} %copy-done.36) | copy-start | bytes 49156
  827.2 16.7 %copy-start.54 = (f32[640]{0:T(1024)S(1)}, f32[640]{0:T(1024)}, u32[]{:S(2)}) copy-start(f32[640]{0:T(1024)} %copy-done.53) | copy-start | bytes 7684
  842.6 24.9 %collective-permute-start.3 = (bf16[8,511,1,256]{3,0,2,1:T(8,128)(2,1)}, bf16[8,511,1,256]{3,0,2,1:T(8,128)(2,1)}, u32[]{:S(2)}, u32[]{:S(2)}) collective-permute-start(bf16[8,511,1,256]{3,0,2,1:T(8,128)(2,1)} %copy.205), channel_id=1, source_target_pairs={{1,0},{2,1},{3,2},{4,3},{5,4},{6,5},{7,6},{8,7},{9,8},{10,9},{11,1... | collective-permute-start | bytes 6279176 | tf_op jit(solution)/shard_map/ppermute | solution.py:148
  913.8 264.5 %copy-start.1 = (bf16[640,2048]{1,0:T(8,128)(2,1)S(1)}, bf16[640,2048]{1,0:T(8,128)(2,1)}, u32[]{:S(2)}) copy-start(bf16[640,2048]{1,0:T(8,128)(2,1)} %param.24) | copy-start | bytes 7864324
  (67 other events, 579.4 us)
where the time goes:
time: 1190 us; the launch traced here: 1180 us
  matrix products  537 us (45%)
  blocking collectives  254 us (21%)
  other arithmetic  196 us (16%)
  local copies, waits for them, and re-layouts  178 us (15%)
  starting transfers between devices  12.3 us (1%)
    psum x1, blocking collectives, local_step(): lax.psum((dw_query, dw_key, dw_value, dw_out, dw_gate, dw_up, dw_down, dg...  254 us
    dot_general x3, matrix products, attend(): jnp.einsum('bnqkgd,bnskd->bnkgqs', q_blk, k_win, preferred_element_type=j...  119 us
    dot_general x3, matrix products, attend(): jnp.einsum('bnkgqs,bnskd->bnqkgd', prob_vals, v_win, preferred_element_ty...  111 us
    dot_general x1, matrix products, local_step(): jnp.einsum('btd,fd->btf', d_down, w_down, preferred_element_type=jnp.floa...  44.6 us
    unnamed x190, local copies, waits for them, and re-layouts  43.8 us
    dot_general x1, matrix products, local_step(): up_proj = jnp.dot(h_mlp, w_up, preferred_element_type=jnp.float32)  33.2 us
    reduce_sum x4, other arithmetic, rms_scale(): values * lax.rsqrt(mean_sq + NORM_EPS)  32.9 us
  transfers between devices with their start and end apart: 5, of which 0 were waited for; matrix products, arithmetic and copies ran while one was open for 18% of the time, Pallas kernels for 0%

commit v1 on v0

v1 whole, which is shorter than its diff:
```python
import functools
import jax
import jax.numpy as jnp
from jax import lax
from jax.experimental import pallas as pl
from jax.experimental.pallas import tpu as pltpu
from jax.sharding import PartitionSpec as P

NORM_EPS = 1e-6
ROPE_BASE = 10000.0
NEG = -1e30
F32 = jnp.float32
BF16 = jnp.bfloat16
VMEM_CAP = 67000000
MESH = pl.DeviceIdType.MESH


def window_size(model_dim):
    return 512 * min(2, 1 + model_dim // 2048)


def score_scale(model_dim, num_heads, head_dim):
    scalar = 256 if head_dim == 256 else model_dim // num_heads
    return scalar ** -0.5


def dot(a, b):
    return jnp.dot(a, b, preferred_element_type=F32)


def dot_nt(a, b):
    return lax.dot_general(a, b, (((1,), (1,)), ((), ())), preferred_element_type=F32)


def unit(v):
    r = lax.rsqrt(jnp.mean(v * v, axis=-1, keepdims=True) + NORM_EPS)
    return v * r, r


def unit_back(n, r, t):
    return r * (t - n * jnp.mean(t * n, axis=-1, keepdims=True))


def rope(n, cos, sin):
    half = n.shape[-1] // 2
    a, b = n[:, :half], n[:, half:]
    return jnp.concatenate([a * cos - b * sin, b * cos + a * sin], axis=-1)


def rope_back(d, cos, sin):
    half = d.shape[-1] // 2
    a, b = d[:, :half], d[:, half:]
    return jnp.concatenate([a * cos + b * sin, b * cos - a * sin], axis=-1)


def gain(ref):
    return 1.0 + ref[...].astype(F32)


def colsum(v):
    return jnp.sum(v, axis=0, keepdims=True)


def kv_kernel(x_ref, cos_ref, sin_ref, wkv_ref, g_in_ref, g_k_ref, kv_ref):
    head = g_k_ref.shape[1]
    n, _ = unit(x_ref[0].astype(F32))
    h = (n * gain(g_in_ref)).astype(BF16)
    proj = dot(h, wkv_ref[...])
    kn, _ = unit(proj[:, :head])
    k = rope(kn * gain(g_k_ref), cos_ref[0], sin_ref[0])
    kv_ref[0, :, :head] = k.astype(BF16)
    kv_ref[0, :, head:] = proj[:, head:].astype(BF16)


def visible_bias(pos_ref, pos_col, first, keys, queries, window, tokens):
    key_pos = pos_col[first:first + keys]
    query_pos = pos_ref[0, :, tokens + first:tokens + first + queries]
    seen = (key_pos > query_pos - window) & (key_pos <= query_pos)
    return jnp.where(seen, 0.0, NEG).astype(F32)


def column_of(row):
    return jnp.transpose(jnp.broadcast_to(row, (8, row.shape[1])))[:, :1]


def main_kernel(window, scale, fchunk,
                x_ref, dy_ref, kv_ref, cos_ref, sin_ref, pos_ref, kv_all,
                wq_ref, wo_ref, wg_ref, wu_ref, wd_ref, g_ai_ref, g_ao_ref, g_mi_ref, g_mo_ref, g_q_ref,
                y_ref, dmid_ref, q_ref, qp_ref, da_ref, lse_ref,
                big_out, kvp_all, dg_out,
                dwg, dwu, dwd, dwo, ga, gb, u_s, o_s, kvp_s, sems, load_sems, send_sems, recv_sems):
    step = pl.program_id(0)
    batch = kv_all.shape[0]
    me, ring = lax.axis_index("cp"), lax.axis_size("cp")
    right, left = lax.rem(me + 1, ring), lax.rem(me + ring - 1, ring)

    def halo(i):
        return pltpu.make_async_remote_copy(
            src_ref=kv_all.at[i], dst_ref=kvp_all.at[i], send_sem=send_sems.at[i], recv_sem=recv_sems.at[i],
            device_id={"cp": right}, device_id_type=MESH)

    def load(i):
        slot = lax.rem(i, 2)
        return pltpu.make_async_copy(kvp_all.at[i], kvp_s.at[slot], load_sems.at[slot])
    last = pl.num_programs(0) - 1
    tokens = x_ref.shape[1]
    head = g_q_ref.shape[1]
    heads = wq_ref.shape[1] // head
    chunks, qc = q_ref.shape[1], q_ref.shape[2] // heads
    keys = window + qc
    ffn = wg_ref.shape[1]

    @pl.when(step == 0)
    def _():
        barrier = pltpu.get_barrier_semaphore()
        for peer in (left, right):
            pl.semaphore_signal(barrier, inc=1, device_id={"cp": peer}, device_id_type=MESH)
        pl.semaphore_wait(barrier, 2)
        for i in range(batch):
            halo(i).start()
        for ref in (dwg, dwu, dwd, dwo, dg_out):
            ref[...] = jnp.zeros_like(ref)
        halo(0).wait_recv()
        load(0).start()

    load(step).wait()
    kvp_ref = kvp_s.at[pl.ds(lax.rem(step, 2), 1)]
    x = x_ref[0].astype(F32)
    n, _ = unit(x)
    h = (n * gain(g_ai_ref)).astype(BF16)
    g_q = gain(g_q_ref)
    pos_col = column_of(pos_ref[0])
    for c in range(chunks):
        rows = slice(c * qc, (c + 1) * qc)
        proj = dot(h[rows], wq_ref[...])
        cos, sin = cos_ref[0, rows], sin_ref[0, rows]
        bias = visible_bias(pos_ref, pos_col, c * qc, keys, qc, window, tokens)
        prev = kvp_ref[0, c * qc:]
        own = kv_ref[0, :(c + 1) * qc]
        k = jnp.concatenate([prev[:, :head], own[:, :head]], axis=0)
        v_t = jnp.transpose(jnp.concatenate([prev[:, head:], own[:, head:]], axis=0))
        for j in range(heads):
            raw = proj[:, j * head:(j + 1) * head]
            qp_ref[0, c, j * qc:(j + 1) * qc] = raw
            qn, _ = unit(raw)
            q = (rope(qn * g_q, cos, sin) * scale).astype(BF16)
            q_ref[0, c, j * qc:(j + 1) * qc] = q
            s = dot_nt(k, q) + bias
            top = jnp.max(s, axis=0, keepdims=True)
            e = jnp.exp(s - top)
            total = jnp.sum(e, axis=0, keepdims=True)
            p = (e * (1.0 / total)).astype(BF16)
            lse_ref[0, c, :, j * qc:(j + 1) * qc] = top + jnp.log(total)
            o_t = dot(v_t, p).astype(BF16)
            o_s[rows, j * head:(j + 1) * head] = jnp.transpose(o_t)

    @pl.when(step < last)
    def _():
        halo(step + 1).wait_recv()
        load(step + 1).start()

    o = o_s[...]
    o_proj = dot(o, wo_ref[...])
    on, o_r = unit(o_proj)
    m = (x + on * gain(g_ao_ref)).astype(BF16).astype(F32)
    mn, m_r = unit(m)
    b = (mn * gain(g_mi_ref)).astype(BF16)
    b_t = jnp.transpose(b)

    down = jnp.zeros_like(x)
    for f in range(ffn // fchunk):
        cols = slice(f * fchunk, (f + 1) * fchunk)
        gate = dot(b, wg_ref[:, cols])
        up = dot(b, wu_ref[:, cols])
        c0 = 0.7978845608028654
        g2 = gate * gate
        t = jnp.tanh(gate * (c0 + (c0 * 0.044715) * g2))
        half = 0.5 * t + 0.5
        act = gate * half
        slope = half + 0.5 * gate * (1.0 - t * t) * (c0 + (3.0 * c0 * 0.044715) * g2)
        ga[:, cols] = act
        gb[:, cols] = slope * up
        u = (act * up).astype(BF16)
        u_s[:, cols] = u
        down = down + dot(u, wd_ref[cols, :])
    dn, d_r = unit(down)
    dy = dy_ref[0].astype(F32)
    y_ref[0] = (m + dn * gain(g_mo_ref)).astype(BF16)
    dg_out[0:1] += colsum(dy * dn)
    d_down = unit_back(dn, d_r, dy * gain(g_mo_ref)).astype(BF16)
    d_down_t = jnp.transpose(d_down)
    d_b = jnp.zeros_like(x)
    for f in range(ffn // fchunk):
        cols = slice(f * fchunk, (f + 1) * fchunk)
        d_hid = dot_nt(d_down, wd_ref[cols, :]).astype(BF16).astype(F32)
        d_up = (d_hid * ga[:, cols]).astype(BF16)
        d_gate = (d_hid * gb[:, cols]).astype(BF16)
        dwd[:, cols] += dot(d_down_t, u_s[:, cols])
        dwg[:, cols] += dot(b_t, d_gate)
        dwu[:, cols] += dot(b_t, d_up)
        d_b = d_b + dot_nt(d_gate, wg_ref[:, cols]) + dot_nt(d_up, wu_ref[:, cols])
    dg_out[1:2] += colsum(d_b * mn)
    d_mid = dy + unit_back(mn, m_r, d_b * gain(g_mi_ref))
    dmid_ref[0] = d_mid
    dg_out[2:3] += colsum(d_mid * on)
    d_o = unit_back(on, o_r, d_mid * gain(g_ao_ref)).astype(BF16)
    dwo[...] += dot(jnp.transpose(d_o), o)
    d_attn = dot_nt(d_o, wo_ref[...]).astype(BF16)
    for c in range(chunks):
        for j in range(heads):
            da_ref[0, c, j * qc:(j + 1) * qc] = d_attn[c * qc:(c + 1) * qc, j * head:(j + 1) * head]

    @pl.when(step == last)
    def _():
        copies, at = [], 0
        for i, part in enumerate((dwg, dwu, dwd, dwo)):
            width = part.shape[1]
            copies.append(pltpu.make_async_copy(part, big_out.at[:, at:at + width], sems.at[i]))
            at += width
        for item in copies:
            item.start()
        for item in copies:
            item.wait()
        for i in range(batch):
            halo(i).wait_send()


def ring_steps(big_ref, core_buf, out_ref, own_v, send_v, recv_v, fin_v,
               core_send, core_recv, load_sem, rs_send, rs_recv, ag_send, ag_recv, p_send, p_recv, fin_sem):
    ring = lax.axis_size("cp")
    me = lax.axis_index("cp")
    n = ring // 2
    z, core = me // 2, lax.rem(me, 2)
    partner = z * 2 + 1 - core
    width = big_ref.shape[3] // 2
    cols = [slice(d * width, (d + 1) * width) for d in range(2)]
    nexts = [lax.rem(z + 1, n) * 2 + core, lax.rem(z + n - 1, n) * 2 + core]

    def rs_chunk(d, s):
        return lax.rem(z + n - s, n) if d == 0 else lax.rem(z + s, n)

    def ag_chunk(d, s):
        return lax.rem(z + 1 + n - s, n) if d == 0 else lax.rem(z + n - 1 + s, n)

    def remote(src, dst, send, recv, device):
        return pltpu.make_async_remote_copy(src_ref=src, dst_ref=dst, send_sem=send, recv_sem=recv,
                                            device_id={"cp": device}, device_id_type=MESH)

    def swap(d, s):
        c = rs_chunk(d, s)
        return remote(big_ref.at[1 - core, c, :, cols[d]], core_buf.at[c, :, cols[d]],
                      core_send.at[d, s], core_recv.at[d, s], partner)

    def loads(d, s):
        c, slot = rs_chunk(d, s), lax.rem(s, 2)
        return (pltpu.make_async_copy(big_ref.at[core, c, :, cols[d]], own_v.at[d, slot, 0], load_sem.at[d, slot, 0]),
                pltpu.make_async_copy(core_buf.at[c, :, cols[d]], own_v.at[d, slot, 1], load_sem.at[d, slot, 1]))

    def rs(d, s):
        return remote(send_v.at[d, lax.rem(s, 2)], recv_v.at[d, s], rs_send.at[d, s], rs_recv.at[d, s], nexts[d])

    def place(d, s):
        return out_ref.at[core, ag_chunk(d, s), :, cols[d]]

    def gather(d, s):
        return remote(place(d, s), place(d, s), ag_send.at[d, s], ag_recv.at[d, s], nexts[d])

    def share(d, s):
        return remote(place(d, s), place(d, s), p_send.at[d, s], p_recv.at[d, s], partner)

    def gather_first(d):
        return remote(fin_v.at[d], place(d, 0), ag_send.at[d, 0], ag_recv.at[d, 0], nexts[d])

    def share_first(d):
        return remote(fin_v.at[d], place(d, 0), p_send.at[d, 0], p_recv.at[d, 0], partner)

    def keep(d):
        return pltpu.make_async_copy(fin_v.at[d], place(d, 0), fin_sem.at[d])

    def start_loads(s):
        for d in range(2):
            swap(d, s).wait_recv()
            for item in loads(d, s):
                item.start()

    def step(u):
        @pl.when(u == 0)
        def _():
            @pl.loop(0, n)
            def _(s):
                for d in range(2):
                    swap(d, s).start()

        @pl.when(u == 1)
        def _():
            start_loads(0)

        s = u - 2

        @pl.when((s >= 0) & (s < n - 1))
        def _():
            for d in range(2):
                for item in loads(d, s):
                    item.wait()
            slot = lax.rem(s, 2)

            @pl.when(s >= 2)
            def _():
                for d in range(2):
                    rs(d, s - 2).wait_send()

            @pl.when(s == 0)
            def _():
                for d in range(2):
                    send_v[d, slot] = (own_v[d, slot, 0] + own_v[d, slot, 1]).astype(BF16)

            @pl.when(s > 0)
            def _():
                for d in range(2):
                    rs(d, s - 1).wait_recv()
                    send_v[d, slot] = (own_v[d, slot, 0] + own_v[d, slot, 1] + recv_v[d, s - 1].astype(F32)).astype(BF16)
            for d in range(2):
                rs(d, s).start()
            start_loads(s + 1)

        @pl.when(s == n - 1)
        def _():
            slot = (n - 1) % 2
            for d in range(2):
                for item in loads(d, n - 1):
                    item.wait()
                rs(d, n - 2).wait_recv()
                fin_v[d] = (own_v[d, slot, 0] + own_v[d, slot, 1] + recv_v[d, n - 2].astype(F32)).astype(BF16)
            for d in range(2):
                gather_first(d).start()
                share_first(d).start()
                keep(d).start()

        g = u - (n + 1)

        @pl.when((g >= 1) & (g < n))
        def _():
            for d in range(2):
                gather(d, g - 1).wait_recv()

            @pl.when(g < n - 1)
            def _():
                for d in range(2):
                    gather(d, g).start()
            for d in range(2):
                share(d, g).start()

        @pl.when(g == n - 1)
        def _():
            for d in range(2):
                keep(d).wait()
                for i in (n - 3, n - 2):
                    rs(d, i).wait_send()

            @pl.loop(0, n)
            def _(i):
                for d in range(2):
                    swap(d, i).wait_send()
                    share(d, i).wait_send()
                    share(d, i).wait_recv()

            @pl.loop(0, n - 1)
            def _(i):
                for d in range(2):
                    gather(d, i).wait_send()

    return step


def back_kernel(window, scale, batch,
                kv_ref, kvp_ref, cos_ref, sin_ref, pos_ref, q_ref, qp_ref, da_ref, lse_ref,
                x_ref, dmid_ref, cosp_ref, sinp_ref, big_ref,
                wqkv_ref, g_ai_ref, g_q_ref, g_k_ref,
                dx_ref, dw_ref, dgi_ref, dgq_ref, dgk_ref, full_ref, core_buf,
                p_s, s_s, ext, d_s, dkv_s, halo_out, halo_in, halo_send, halo_recv, *ring_refs):
    step = pl.program_id(0)
    tokens = x_ref.shape[1]
    head = g_q_ref.shape[1]
    chunks = q_ref.shape[1]
    q_dim = wqkv_ref.shape[1] - dkv_s.shape[2]
    heads = q_dim // head
    qc = q_ref.shape[2] // heads
    keys = window + qc
    me, ring = lax.axis_index("cp"), lax.axis_size("cp")
    left = lax.rem(me + ring - 1, ring)
    ring_step = ring_steps(big_ref, core_buf, full_ref, *ring_refs)

    def halo(i):
        slot = lax.rem(i, 2)
        return pltpu.make_async_remote_copy(
            src_ref=halo_out.at[slot], dst_ref=halo_in.at[i], send_sem=halo_send.at[slot], recv_sem=halo_recv.at[i],
            device_id={"cp": left}, device_id_type=MESH)

    @pl.when(step == 0)
    def _():
        barrier = pltpu.get_barrier_semaphore()
        for hop in (1, 2, ring - 1, ring - 2):
            pl.semaphore_signal(barrier, inc=1, device_id={"cp": lax.rem(me + hop, ring)}, device_id_type=MESH)
        pl.semaphore_wait(barrier, 4)
        for ref in (dw_ref, dgi_ref, dgq_ref, dgk_ref):
            ref[...] = jnp.zeros_like(ref)

    ring_step(2 * step)

    def attend(c):
        g_q = gain(g_q_ref)
        pos_col = column_of(pos_ref[0])
        rows = slice(c * qc, (c + 1) * qc)
        slot = lax.rem(step, 2)
        cos, sin = cos_ref[0, rows], sin_ref[0, rows]
        bias = visible_bias(pos_ref, pos_col, c * qc, keys, qc, window, tokens)
        prev = kvp_ref[0, c * qc:]
        own = kv_ref[0, :(c + 1) * qc]
        k = jnp.concatenate([prev[:, :head], own[:, :head]], axis=0)
        v = jnp.concatenate([prev[:, head:], own[:, head:]], axis=0)
        k_t = jnp.transpose(k)
        dg = jnp.zeros((1, head), F32)
        for j in range(heads):
            lanes = slice(j * qc, (j + 1) * qc)
            q = q_ref[0, c, lanes]
            d_o = da_ref[0, c, lanes]
            s = dot_nt(k, q) + bias
            p = jnp.exp(s - lse_ref[0, c, :, lanes])
            d_p = dot_nt(v, d_o)
            delta = jnp.sum(d_p * p, axis=0, keepdims=True)
            d_sc = (p * (d_p - delta)).astype(BF16)
            p_s[:, lanes] = p.astype(BF16)
            s_s[:, lanes] = d_sc
            d_q = jnp.transpose(dot(k_t, d_sc)) * scale
            qn, q_r = unit(qp_ref[0, c, lanes])
            d_qn = rope_back(d_q, cos, sin)
            dg = dg + colsum(d_qn * qn)
            d_s[slot, rows, j * head:(j + 1) * head] = unit_back(qn, q_r, d_qn * g_q).astype(BF16)
        dgq_ref[...] += dg
        span = slice(c * qc, c * qc + keys)
        d_k = dot(s_s[...], q_ref[0, c])
        d_v = dot(p_s[...], da_ref[0, c])
        if c == 0:
            ext[span, :head] = d_k
            ext[span, head:] = d_v
            ext[keys:] = jnp.zeros_like(ext[keys:])
        else:
            ext[span, :head] += d_k
            ext[span, head:] += d_v

    @pl.when(step < batch)
    def _():
        attend(0)

    ring_step(2 * step + 1)

    @pl.when(step < batch)
    def _():
        for c in range(1, chunks):
            attend(c)
        slot = lax.rem(step, 2)

        @pl.when(step >= 2)
        def _():
            halo(step - 2).wait_send()
        halo_out[slot] = ext[:window].astype(BF16)
        dkv_s[slot] = ext[window:]
        halo(step).start()

    @pl.when(step > 0)
    def _():
        slot = lax.rem(step + 1, 2)
        n, r = unit(x_ref[0].astype(F32))
        g_ai = gain(g_ai_ref)
        h = (n * g_ai).astype(BF16)
        kn, k_r = unit(dot(h, wqkv_ref[:, q_dim:q_dim + head]))
        halo(step - 1).wait_recv()
        total = dkv_s[slot] + halo_in[step - 1].astype(F32)
        d_kn = rope_back(total[:, :head], cosp_ref[0], sinp_ref[0])
        dgk_ref[...] += colsum(d_kn * kn)
        d_s[slot, :, q_dim:q_dim + head] = unit_back(kn, k_r, d_kn * gain(g_k_ref)).astype(BF16)
        d_s[slot, :, q_dim + head:] = total[:, head:].astype(BF16)
        d_all = d_s[slot]
        dw_ref[...] += dot(jnp.transpose(h), d_all)
        d_h = dot_nt(d_all, wqkv_ref[...])
        dgi_ref[...] += colsum(d_h * n)
        dx_ref[0] = (dmid_ref[0] + unit_back(n, r, d_h * g_ai)).astype(BF16)

    @pl.when(step == batch)
    def _():
        halo(batch - 2).wait_send()
        halo(batch - 1).wait_send()


def per_seq(shape, lag=None, **kw):
    tail = tuple(shape[1:])
    top = shape[0] - 1
    if lag is None:
        return pl.BlockSpec((1,) + tail, lambda b: (b,) + (0,) * len(tail), **kw)
    return pl.BlockSpec((1,) + tail, lambda b: (jnp.clip(b - lag, 0, top),) + (0,) * len(tail), **kw)


def whole(shape):
    return pl.BlockSpec(tuple(shape), lambda b: (0,) * len(shape), pipeline_mode=pl.Buffered(1))


ANY = pl.BlockSpec(memory_space=pl.ANY)


def call(kernel, steps, ins, in_specs, outs, out_specs, scratch, flops, **params):
    nbytes = sum(a.size * a.dtype.itemsize for a in ins) + sum(o.size * o.dtype.itemsize for o in outs)
    return pl.pallas_call(
        kernel, grid=(steps,), in_specs=in_specs, out_specs=out_specs, out_shape=outs, scratch_shapes=scratch,
        compiler_params=pltpu.CompilerParams(dimension_semantics=("arbitrary",), vmem_limit_bytes=VMEM_CAP, **params),
        cost_estimate=pl.CostEstimate(flops=flops, bytes_accessed=nbytes, transcendentals=0),
    )(*ins)


def solution(mesh):
    cp_size = mesh.shape["cp"]
    to_next = [(idx, idx + 1) for idx in range(cp_size - 1)]

    def local_step(x, dy, positions, w_query, w_key, w_value, w_out, w_gate, w_up, w_down, g_attn_in, g_attn_out, g_mlp_in, g_mlp_out, g_query, g_key):
        n_batch, tokens, dim = x.shape
        head = g_query.shape[0]
        q_dim = w_query.shape[1]
        kv_dim = w_key.shape[1] + w_value.shape[1]
        heads = q_dim // head
        ffn = w_gate.shape[1]
        window = window_size(dim)
        scale = score_scale(dim, heads, head)
        qc = min(256, tokens)
        chunks = tokens // qc
        keys = window + qc
        shard_idx = lax.axis_index("cp")
        sds = jax.ShapeDtypeStruct
        n_tok = n_batch * tokens
        chips = cp_size // 2
        wide = 3 * ffn + q_dim
        slab = dim // cp_size
        dma = pltpu.SemaphoreType.DMA

        half = head // 2
        inv_freq = ROPE_BASE ** (-2.0 * jnp.arange(half, dtype=F32) / head)
        angles = positions.astype(F32)[..., None] * inv_freq
        cos, sin = jnp.cos(angles), jnp.sin(angles)
        row = lambda g: g.reshape(1, -1)
        w_kv = jnp.concatenate([w_key, w_value], axis=1)
        w_qkv = jnp.concatenate([w_query, w_kv], axis=1)
        g_ai, g_ao, g_mi, g_mo, g_q, g_k = map(row, (g_attn_in, g_attn_out, g_mlp_in, g_mlp_out, g_query, g_key))
        pos_prev = lax.ppermute(positions, "cp", to_next)
        pos_prev = jnp.where(shard_idx > 0, pos_prev, -(2 ** 30))
        pos_ext = jnp.concatenate([pos_prev, positions], axis=1)[:, None, :]
        cs = per_seq(cos.shape)

        (kv,) = call(kv_kernel, n_batch, [x, cos, sin, w_kv, g_ai, g_k],
                     [per_seq(x.shape), cs, cs, whole(w_kv.shape), whole(g_ai.shape), whole(g_k.shape)],
                     [sds((n_batch, tokens, kv_dim), BF16)], [per_seq((n_batch, tokens, kv_dim))], [], 2 * n_tok * dim * kv_dim)

        stack = (n_batch, chunks, heads * qc, head)
        weights = [w_query, w_out, w_gate, w_up, w_down, g_ai, g_ao, g_mi, g_mo, g_q]
        lse_shape = (n_batch, chunks, 1, heads * qc)
        xs = per_seq(x.shape)
        y, d_mid, q_st, qp_st, da_st, lse, big, kv_prev, dg_main = call(
            functools.partial(main_kernel, window, scale, 512), n_batch,
            [x, dy, kv, cos, sin, pos_ext, kv] + weights,
            [xs, xs, per_seq(kv.shape), cs, cs, per_seq(pos_ext.shape), ANY] + [whole(w.shape) for w in weights],
            [sds(x.shape, BF16), sds(x.shape, F32), sds(stack, BF16), sds(stack, F32), sds(stack, BF16), sds(lse_shape, F32),
             sds((dim, wide), F32), sds(kv.shape, BF16), sds((8, dim), F32)],
            [xs, xs, per_seq(stack), per_seq(stack, pipeline_mode=pl.Buffered(1)), per_seq(stack), per_seq(lse_shape),
             ANY, ANY, whole((8, dim))],
            [pltpu.VMEM((dim, ffn), F32)] * 3 + [pltpu.VMEM((dim, q_dim), F32)]
            + [pltpu.VMEM((tokens, ffn), F32)] * 2 + [pltpu.VMEM((tokens, ffn), BF16), pltpu.VMEM((tokens, q_dim), BF16),
                                                     pltpu.VMEM((2, tokens, kv_dim), BF16),
                                                     dma((4,)), dma((2,)), dma((n_batch,)), dma((n_batch,))],
            2 * n_tok * (9 * dim * ffn + 4 * dim * q_dim + 2 * q_dim * keys),
            collective_id=0, has_side_effects=True)

        big = big.reshape(2, chips, slab, wide)
        part = (slab, wide // 2)
        first, behind = (lambda a: per_seq(a.shape, 0)), (lambda a: per_seq(a.shape, 1))
        seq_in = [kv, kv_prev, cos, sin, pos_ext, q_st, qp_st, da_st, lse]
        lag_in = [x, d_mid, cos, sin]
        back_w = [w_qkv, g_ai, g_q, g_k]
        dx, dw, dgi, dgq, dgk, full, _ = call(
            functools.partial(back_kernel, window, scale, n_batch), n_batch + 1,
            seq_in + lag_in + [big] + back_w,
            [first(a) for a in seq_in] + [behind(a) for a in lag_in] + [ANY] + [whole(w.shape) for w in back_w],
            [sds(x.shape, BF16), sds(w_qkv.shape, F32), sds((1, dim), F32), sds((1, head), F32), sds((1, head), F32),
             sds(big.shape, BF16), sds(big.shape[1:], F32)],
            [behind(x), whole(w_qkv.shape), whole((1, dim)), whole((1, head)), whole((1, head)), ANY, ANY],
            [pltpu.VMEM((keys, heads * qc), BF16)] * 2
            + [pltpu.VMEM((window + tokens, kv_dim), F32), pltpu.VMEM((2, tokens, q_dim + kv_dim), BF16),
               pltpu.VMEM((2, tokens, kv_dim), F32), pltpu.VMEM((2, window, kv_dim), BF16),
               pltpu.VMEM((n_batch, window, kv_dim), BF16), dma((2,)), dma((n_batch,)),
               pltpu.VMEM((2, 2, 2) + part, F32), pltpu.VMEM((2, 2) + part, BF16),
               pltpu.VMEM((2, chips - 1) + part, BF16), pltpu.VMEM((2,) + part, BF16),
               dma((2, chips)), dma((2, chips)), dma((2, 2, 2)), dma((2, chips - 1)), dma((2, chips - 1)),
               dma((2, chips - 1)), dma((2, chips - 1)), dma((2, chips)), dma((2, chips)), dma((2,))],
            2 * n_tok * (2 * dim * (q_dim + kv_dim) + 5 * q_dim * keys),
            collective_id=1, has_side_effects=True)

        full = full.reshape(dim, wide)
        r_dw, r_dg, r_dgq, r_dgi, r_dgk = lax.psum((dw, dg_main, dgq, dgi, dgk), "cp")
        b16 = lambda v: v.astype(BF16)
        kv_half = q_dim + kv_dim // 2
        return (y, dx, b16(r_dw[:, :q_dim]), b16(r_dw[:, q_dim:kv_half]), b16(r_dw[:, kv_half:]), full[:, 3 * ffn:].T,
                full[:, :ffn], full[:, ffn:2 * ffn], full[:, 2 * ffn:3 * ffn].T,
                b16(r_dgi[0]), b16(r_dg[2]), b16(r_dg[1]), b16(r_dg[0]), b16(r_dgq[0]), b16(r_dgk[0]))

    seq_spec = P("dp", "cp", None)
    in_specs = (seq_spec, seq_spec, P("dp", "cp")) + (P(None, None),) * 7 + (P(None),) * 6
    out_specs = (seq_spec, seq_spec) + (P("dp", None),) * 7 + (P("dp"),) * 6
    return jax.shard_map(local_step, mesh=mesh, in_specs=in_specs, out_specs=out_specs, check_vma=False)
```

time: 1190 us -> 560 us (0.47)
  matrix products: 537 us -> 0 us
  Pallas kernels: 0 us -> 439 us
  blocking collectives: 254 us -> 66.8 us
  other arithmetic: 196 us -> 14.4 us
  local copies, waits for them, and re-layouts: 178 us -> 33.1 us
    dot_general x27 -> x0, matrix products: 537 us -> none  [the longest x3 119 us: attend(): jnp.einsum('bnqkgd,bnskd->bnkgqs', q_blk, k_win, preferred_element_type=j...]
    pallas_call x0 -> x3, Pallas kernels: none -> 439 us  [call(): pl.pallas_call(kernel, grid=(steps,), in_specs=in_specs, out_specs=out_sp...]
    psum x1, blocking collectives: 254 us -> 66.8 us  [local_step(): lax.psum((dw, dg_main, dgq, dgi, dgk), 'cp')]
    reduce_sum x8 -> x0, other arithmetic: 74.2 us -> none  [the longest x4 32.9 us: rms_scale(): values * lax.rsqrt(mean_sq + NORM_EPS)]
    reshape x4 -> x6, local copies, waits for them, and re-layouts: 51.8 us -> 6.12 us  [local_step(): row = lambda g: g.reshape(1, -1)]
    unnamed x190 -> x22, local copies, waits for them, and re-layouts: 43.8 us -> 13 us
    convert_element_type x4 -> x1, other arithmetic: 31.3 us -> 0.72 us  [local_step(): angles = positions.astype(F32)[..., None] * inv_freq]
    slice x15 -> x4, local copies, waits for them, and re-layouts: 33.8 us -> 10.3 us  [the longest x1 5.25 us: local_step(): full[:, 2 * ffn:3 * ffn]]
  transfers between devices with their start and end apart: 5 -> 1, of which waited for: 0 -> 0; matrix products, arithmetic and copies ran while one was open for 18% -> 4% of each run, Pallas kernels for 0% -> 2%
where the time goes in v1:
time: 560 us; the launch traced here: 557 us
  Pallas kernels  439 us (78%)
  blocking collectives  66.8 us (12%)
  local copies, waits for them, and re-layouts  33.1 us (6%)
  other arithmetic  14.4 us (3%)
    pallas_call x3, Pallas kernels, call(): pl.pallas_call(kernel, grid=(steps,), in_specs=in_specs, out_specs=out_sp...  439 us
    psum x1, blocking collectives, local_step(): lax.psum((dw, dg_main, dgq, dgi, dgk), 'cp')  66.8 us
    unnamed x22, local copies, waits for them, and re-layouts  13 us
  transfers between devices with their start and end apart: 1, of which 0 were waited for; matrix products, arithmetic and copies ran while one was open for 4% of the time, Pallas kernels for 2%

profile of v1, /device:TPU:30, one launch (start us, length us, event | category | flops | bytes accessed | tf_op | source)
XLA Modules:
  0.0 556.5 jit_solution(12169185261975431470)
XLA Ops:
  0.6 1.8 collective-permute-start
  2.5 0.7 convert_element_type.36
  3.2 1.2 reshape.67.g_k_ref
  4.4 1.3 reshape.66.g_in_ref.g_ai_ref
  5.7 2.0 pad_maximum_fusion.1.wkv_ref
  7.7 2.9 pad_maximum_fusion.wqkv_ref
  10.6 8.8 %multiply_sine_fusion = (f32[8,512,128]{2,1,0:T(8,128)}, f32[8,512,128]{2,1,0:T(8,128)}) fusion(f32[128]{0:T(128)S(1)} %multiply_power_fusion, f32[8,512]{1,0:T(8,128)S(1)} %convert_element_type.36), kind=kLoop, calls=%fused_computation | loop fusion | flops 524288 | bytes 4211200 | tf_op jit(solution)/shard_map/sin | solution.py:546
  19.4 10.7 %shard_map.271.kv_ref.kv_all = bf16[8,512,512]{2,1,0:T(8,128)(2,1)} custom-call(bf16[8,512,640]{2,1,0:T(8,128)(2,1)} %x_ref.5, f32[8,512,128]{2,1,0:T(8,128)} %get-tuple-element.74.cos_ref.cosp_ref, f32[8,512,128]{2,1,0:T(8,128)} %get-tuple-element.73.sin_ref.sinp_ref, bf16[640,512]{1,0:T(8,128)(2,1)} %pad_maximum_fusion.1.wkv_ref, ...), custom_call_target="tpu_custom_call" | custom-call | flops 2684354560 | bytes 14288640 | tf_op jit(solution)/shard_map/pallas_call | solution.py:512
  30.1 1.2 reshape.71.g_q_ref
  31.3 0.0 copy-done.3
  31.3 0.6 reshape.68.g_ao_ref
  31.9 0.0 copy-done.4
  31.9 0.6 reshape.69.g_mi_ref
  32.5 1.3 reshape.70.g_mo_ref
  33.8 0.0 collective-permute-done
  33.8 0.0 copy-done
  33.8 0.6 broadcast_in_dim.10.pos_ref
  34.4 260.4 %shard_map.272 = (bf16[8,512,640]{2,1,0:T(8,128)(2,1)}, f32[8,512,640]{2,1,0:T(8,128)}, bf16[8,2,1024,256]{3,2,1,0:T(8,128)(2,1)}, f32[8,2,1024,256]{3,2,1,0:T(8...) custom-call(bf16[8,512,640]{2,1,0:T(8,128)(2,1)} %x_ref.5, ...), custom_call_target="tpu_custom_call" | custom-call | flops 130996502528 | bytes 105506304 | tf_op jit(solution)/shard_map/pallas_call | solution.py:512
  294.8 168.4 %shard_map.273 = (bf16[8,512,640]{2,1,0:T(8,128)(2,1)}, f32[640,1536]{1,0:T(8,128)}, f32[1,640]{1,0:T(1,128)}, f32[1,256]{1,0:T(1,128)}, f32[1,256]{1,0:T(1,128)...) custom-call(bf16[8,512,512]{2,1,0:T(8,128)(2,1)} %shard_map.271.kv_ref.kv_all, ...), custom_call_target="tpu_custom_call" | custom-call | flops 48318382080 | bytes 114006784 | tf_op jit(solution)/shard_map/pallas_call | solution.py:512
  463.2 2.5 slice_bitcast_fusion
  465.7 5.3 fusion
  470.9 0.0 copy-done.1
  470.9 0.0 copy-done.2
  471.0 66.8 %all-reduce.2 = (bf16[640,1536]{1,0:T(8,128)(2,1)}, bf16[1,640]{1,0:T(2,128)(2,1)S(1)}, bf16[8,640]{1,0:T(8,128)(2,1)S(1)}, bf16[1,256]{1,0:T(2,128)(2,1)S(1)}, bf16[1,256]{1,0:T(2,128)(2,1)S(1)}) all-reduce(f32[640,1536]{1,0:T(8,128)} %get-tuple-element.39, f32[1,640]{1,0:T(1,128)S(1)} %copy-done.2, ...), channel_id=1, replica_groups=mesh['dp'=4,'cp'=16] {'cp'}, use_global_device_ids=true, to_apply=%region_0.1 | all-reduce | flops 989312 | bytes 5935872 | tf_op jit(solution)/shard_map/psum | solution.py:604
  537.7 2.0 fusion.1
  539.7 2.5 slice.46
  542.2 2.6 copy.33
  544.7 2.5 copy.32
  547.2 0.6 slice_reduce_fusion
  547.8 0.5 convert_reduce_fusion.1
  548.4 5.5 copy.46
  553.9 2.4 copy.47
  (17 shorter events, 0.0 us)
Async XLA Ops:
  0.6 33.1 %collective-permute-start = (s32[8,512]{1,0:T(8,128)}, s32[8,512]{1,0:T(8,128)S(1)}, u32[]{:S(2)}, u32[]{:S(2)}) collective-permute-start(s32[8,512]{1,0:T(8,128)} %param.18), channel_id=1, source_target_pairs={{0,1},{1,2},{2,3},{3,4},{4,5},{5,6},{6,7},{7,8},{8,9},{9,10},{10,1... | collective-permute-start | bytes 49160 | tf_op jit(solution)/shard_map/ppermute | solution.py:551
  19.4 11.9 %copy-start.3 = (bf16[640]{0:T(1024)(128)(2,1)S(1)}, bf16[640]{0:T(1024)(128)(2,1)}, u32[]{:S(2)}) copy-start(bf16[640]{0:T(1024)(128)(2,1)} %param.27) | copy-start | bytes 3844
  19.4 12.5 %copy-start.4 = (bf16[640]{0:T(1024)(128)(2,1)S(1)}, bf16[640]{0:T(1024)(128)(2,1)}, u32[]{:S(2)}) copy-start(bf16[640]{0:T(1024)(128)(2,1)} %param.28) | copy-start | bytes 3844
  19.4 14.4 %copy-start = (s32[8,512]{1,0:T(8,128)S(1)}, s32[8,512]{1,0:T(8,128)}, u32[]{:S(2)}) copy-start(s32[8,512]{1,0:T(8,128)} %param.18) | copy-start | bytes 49156
  465.7 5.3 copy-start.1
  465.7 5.3 copy-start.2
  465.7 5.3 copy-start.5
  465.7 5.3 copy-start.6
  544.7 9.2 %slice-start = ((s8[5242880]{0:T(1024)(128)(4,1)}), s8[1048576]{0:T(1024)(128)(4,1)S(1)}, s32[]{:S(2)}) async-start(s8[5242880]{0:T(1024)(128)(4,1)} %bitcast.7), calls=%async_computation | async-start | bytes 2097152
  548.4 5.6 slice-start.1

commit v2 on v1

--- a/solution.py
+++ b/solution.py
@@ -53,23 +53,27 @@
     return jnp.concatenate([a * cos + b * sin, b * cos - a * sin], axis=-1)
 
 
+def gains(ref, dim, head, *rows):
+    return [ref.at[i:i + 1, :dim if i < 4 else head] for i in rows]
+
+
 def gain(ref):
-    return 1.0 + ref[...].astype(F32)
+    return 1.0 + ref[...]
 
 
 def colsum(v):
     return jnp.sum(v, axis=0, keepdims=True)
 
 
-def kv_kernel(x_ref, cos_ref, sin_ref, wkv_ref, g_in_ref, g_k_ref, kv_ref):
-    head = g_k_ref.shape[1]
+def kv_kernel(x_ref, cos_ref, sin_ref, wk_ref, wv_ref, g_ref, kv_ref):
+    head = wk_ref.shape[1]
+    g_in_ref, g_k_ref = gains(g_ref, x_ref.shape[2], head, 0, 5)
     n, _ = unit(x_ref[0].astype(F32))
     h = (n * gain(g_in_ref)).astype(BF16)
-    proj = dot(h, wkv_ref[...])
-    kn, _ = unit(proj[:, :head])
+    kn, _ = unit(dot(h, wk_ref[...]))
     k = rope(kn * gain(g_k_ref), cos_ref[0], sin_ref[0])
     kv_ref[0, :, :head] = k.astype(BF16)
-    kv_ref[0, :, head:] = proj[:, head:].astype(BF16)
+    kv_ref[0, :, head:] = dot(h, wv_ref[...]).astype(BF16)
 
 
 def visible_bias(pos_ref, pos_col, first, keys, queries, window, tokens):
@@ -85,7 +89,7 @@
 
 def main_kernel(window, scale, fchunk,
                 x_ref, dy_ref, kv_ref, cos_ref, sin_ref, pos_ref, kv_all,
-                wq_ref, wo_ref, wg_ref, wu_ref, wd_ref, g_ai_ref, g_ao_ref, g_mi_ref, g_mo_ref, g_q_ref,
+                wq_ref, wo_ref, wg_ref, wu_ref, wd_ref, g_ref,
                 y_ref, dmid_ref, q_ref, qp_ref, da_ref, lse_ref,
                 big_out, kvp_all, dg_out,
                 dwg, dwu, dwd, dwo, ga, gb, u_s, o_s, kvp_s, sems, load_sems, send_sems, recv_sems):
@@ -104,7 +108,8 @@
         return pltpu.make_async_copy(kvp_all.at[i], kvp_s.at[slot], load_sems.at[slot])
     last = pl.num_programs(0) - 1
     tokens = x_ref.shape[1]
-    head = g_q_ref.shape[1]
+    head = q_ref.shape[3]
+    g_ai_ref, g_ao_ref, g_mi_ref, g_mo_ref, g_q_ref = gains(g_ref, x_ref.shape[2], head, 0, 1, 2, 3, 4)
     heads = wq_ref.shape[1] // head
     chunks, qc = q_ref.shape[1], q_ref.shape[2] // heads
     keys = window + qc
@@ -167,9 +172,12 @@
     b = (mn * gain(g_mi_ref)).astype(BF16)
     b_t = jnp.transpose(b)
 
-    down = jnp.zeros_like(x)
-    for f in range(ffn // fchunk):
-        cols = slice(f * fchunk, (f + 1) * fchunk)
+    acc = dmid_ref.at[0]
+    acc[...] = jnp.zeros_like(x)
+
+    @pl.loop(0, ffn // fchunk)
+    def _(f):
+        cols = pl.ds(pl.multiple_of(f * fchunk, fchunk), fchunk)
         gate = dot(b, wg_ref[:, cols])
         up = dot(b, wu_ref[:, cols])
         c0 = 0.7978845608028654
@@ -182,23 +190,29 @@
         gb[:, cols] = slope * up
         u = (act * up).astype(BF16)
         u_s[:, cols] = u
-        down = down + dot(u, wd_ref[cols, :])
+        acc[...] += dot(u, wd_ref[cols, :])
+
+    down = acc[...]
     dn, d_r = unit(down)
     dy = dy_ref[0].astype(F32)
     y_ref[0] = (m + dn * gain(g_mo_ref)).astype(BF16)
     dg_out[0:1] += colsum(dy * dn)
     d_down = unit_back(dn, d_r, dy * gain(g_mo_ref)).astype(BF16)
     d_down_t = jnp.transpose(d_down)
-    d_b = jnp.zeros_like(x)
-    for f in range(ffn // fchunk):
-        cols = slice(f * fchunk, (f + 1) * fchunk)
+    acc[...] = jnp.zeros_like(x)
+
+    @pl.loop(0, ffn // fchunk)
+    def _(f):
+        cols = pl.ds(pl.multiple_of(f * fchunk, fchunk), fchunk)
         d_hid = dot_nt(d_down, wd_ref[cols, :]).astype(BF16).astype(F32)
         d_up = (d_hid * ga[:, cols]).astype(BF16)
         d_gate = (d_hid * gb[:, cols]).astype(BF16)
         dwd[:, cols] += dot(d_down_t, u_s[:, cols])
         dwg[:, cols] += dot(b_t, d_gate)
         dwu[:, cols] += dot(b_t, d_up)
-        d_b = d_b + dot_nt(d_gate, wg_ref[:, cols]) + dot_nt(d_up, wu_ref[:, cols])
+        acc[...] += dot_nt(d_gate, wg_ref[:, cols]) + dot_nt(d_up, wu_ref[:, cols])
+
+    d_b = acc[...]
     dg_out[1:2] += colsum(d_b * mn)
     d_mid = dy + unit_back(mn, m_r, d_b * gain(g_mi_ref))
     dmid_ref[0] = d_mid
@@ -225,15 +239,14 @@
             halo(i).wait_send()
 
 
-def ring_steps(big_ref, core_buf, out_ref, own_v, send_v, recv_v, fin_v,
+def ring_steps(cols, big_ref, core_buf, out_ref, own_v, send_v, recv_v, fin_v,
                core_send, core_recv, load_sem, rs_send, rs_recv, ag_send, ag_recv, p_send, p_recv, fin_sem):
     ring = lax.axis_size("cp")
     me = lax.axis_index("cp")
     n = ring // 2
     z, core = me // 2, lax.rem(me, 2)
     partner = z * 2 + 1 - core
-    width = big_ref.shape[3] // 2
-    cols = [slice(d * width, (d + 1) * width) for d in range(2)]
+    part = [slice(0, c.stop - c.start) for c in cols]
     nexts = [lax.rem(z + 1, n) * 2 + core, lax.rem(z + n - 1, n) * 2 + core]
 
     def rs_chunk(d, s):
@@ -253,11 +266,11 @@
 
     def loads(d, s):
         c, slot = rs_chunk(d, s), lax.rem(s, 2)
-        return (pltpu.make_async_copy(big_ref.at[core, c, :, cols[d]], own_v.at[d, slot, 0], load_sem.at[d, slot, 0]),
-                pltpu.make_async_copy(core_buf.at[c, :, cols[d]], own_v.at[d, slot, 1], load_sem.at[d, slot, 1]))
+        return (pltpu.make_async_copy(big_ref.at[core, c, :, cols[d]], own_v.at[d, slot, 0, :, part[d]], load_sem.at[d, slot, 0]),
+                pltpu.make_async_copy(core_buf.at[c, :, cols[d]], own_v.at[d, slot, 1, :, part[d]], load_sem.at[d, slot, 1]))
 
     def rs(d, s):
-        return remote(send_v.at[d, lax.rem(s, 2)], recv_v.at[d, s], rs_send.at[d, s], rs_recv.at[d, s], nexts[d])
+        return remote(send_v.at[d, lax.rem(s, 2), :, part[d]], recv_v.at[d, s, :, part[d]], rs_send.at[d, s], rs_recv.at[d, s], nexts[d])
 
     def place(d, s):
         return out_ref.at[core, ag_chunk(d, s), :, cols[d]]
@@ -269,13 +282,13 @@
         return remote(place(d, s), place(d, s), p_send.at[d, s], p_recv.at[d, s], partner)
 
     def gather_first(d):
-        return remote(fin_v.at[d], place(d, 0), ag_send.at[d, 0], ag_recv.at[d, 0], nexts[d])
+        return remote(fin_v.at[d, :, part[d]], place(d, 0), ag_send.at[d, 0], ag_recv.at[d, 0], nexts[d])
 
     def share_first(d):
-        return remote(fin_v.at[d], place(d, 0), p_send.at[d, 0], p_recv.at[d, 0], partner)
+        return remote(fin_v.at[d, :, part[d]], place(d, 0), p_send.at[d, 0], p_recv.at[d, 0], partner)
 
     def keep(d):
-        return pltpu.make_async_copy(fin_v.at[d], place(d, 0), fin_sem.at[d])
+        return pltpu.make_async_copy(fin_v.at[d, :, part[d]], place(d, 0), fin_sem.at[d])
 
     def start_loads(s):
         for d in range(2):
@@ -312,13 +325,16 @@
             @pl.when(s == 0)
             def _():
                 for d in range(2):
-                    send_v[d, slot] = (own_v[d, slot, 0] + own_v[d, slot, 1]).astype(BF16)
+                    w = part[d]
+                    send_v[d, slot, :, w] = (own_v[d, slot, 0, :, w] + own_v[d, slot, 1, :, w]).astype(BF16)
 
             @pl.when(s > 0)
             def _():
                 for d in range(2):
                     rs(d, s - 1).wait_recv()
-                    send_v[d, slot] = (own_v[d, slot, 0] + own_v[d, slot, 1] + recv_v[d, s - 1].astype(F32)).astype(BF16)
+                    w = part[d]
+                    send_v[d, slot, :, w] = (own_v[d, slot, 0, :, w] + own_v[d, slot, 1, :, w]
+                                             + recv_v[d, s - 1, :, w].astype(F32)).astype(BF16)
             for d in range(2):
                 rs(d, s).start()
             start_loads(s + 1)
@@ -330,7 +346,9 @@
                 for item in loads(d, n - 1):
                     item.wait()
                 rs(d, n - 2).wait_recv()
-                fin_v[d] = (own_v[d, slot, 0] + own_v[d, slot, 1] + recv_v[d, n - 2].astype(F32)).astype(BF16)
+                w = part[d]
+                fin_v[d, :, w] = (own_v[d, slot, 0, :, w] + own_v[d, slot, 1, :, w]
+                                  + recv_v[d, n - 2, :, w].astype(F32)).astype(BF16)
             for d in range(2):
                 gather_first(d).start()
                 share_first(d).start()
@@ -372,28 +390,42 @@
     return step
 
 
+def piece_widths(wide):
+    tiles = wide // 128
+    down = tiles * 5 // 28
+    return (tiles // 2 - down) * 128, down * 128
+
+
 def back_kernel(window, scale, batch,
                 kv_ref, kvp_ref, cos_ref, sin_ref, pos_ref, q_ref, qp_ref, da_ref, lse_ref,
                 x_ref, dmid_ref, cosp_ref, sinp_ref, big_ref,
-                wqkv_ref, g_ai_ref, g_q_ref, g_k_ref,
+                wq_ref, wk_ref, wv_ref, g_ref,
                 dx_ref, dw_ref, dgi_ref, dgq_ref, dgk_ref, full_ref, core_buf,
                 p_s, s_s, ext, d_s, dkv_s, halo_out, halo_in, halo_send, halo_recv, *ring_refs):
     step = pl.program_id(0)
     tokens = x_ref.shape[1]
-    head = g_q_ref.shape[1]
+    head = q_ref.shape[3]
+    g_ai_ref, g_q_ref, g_k_ref = gains(g_ref, x_ref.shape[2], head, 0, 4, 5)
     chunks = q_ref.shape[1]
-    q_dim = wqkv_ref.shape[1] - dkv_s.shape[2]
+    q_dim = wq_ref.shape[1]
     heads = q_dim // head
     qc = q_ref.shape[2] // heads
     keys = window + qc
     me, ring = lax.axis_index("cp"), lax.axis_size("cp")
     left = lax.rem(me + ring - 1, ring)
-    ring_step = ring_steps(big_ref, core_buf, full_ref, *ring_refs)
-
-    def halo(i):
+    per_ring = len(ring_refs) // 2
+    up_w, down_w = piece_widths(big_ref.shape[3])
+    ring_a, ring_b = [
+        ring_steps([slice(i * up_w, (i + 1) * up_w), slice(2 * up_w + i * down_w, 2 * up_w + (i + 1) * down_w)],
+                   big_ref, core_buf, full_ref, *ring_refs[i * per_ring:(i + 1) * per_ring])
+        for i in range(2)]
+
+    def halo(i, part):
         slot = lax.rem(i, 2)
+        cols = slice(part * head, (part + 1) * head)
         return pltpu.make_async_remote_copy(
-            src_ref=halo_out.at[slot], dst_ref=halo_in.at[i], send_sem=halo_send.at[slot], recv_sem=halo_recv.at[i],
+            src_ref=halo_out.at[slot, :, cols], dst_ref=halo_in.at[i, :, cols],
+            send_sem=halo_send.at[slot, part], recv_sem=halo_recv.at[i, part],
             device_id={"cp": left}, device_id_type=MESH)
 
     @pl.when(step == 0)
@@ -405,7 +437,8 @@
         for ref in (dw_ref, dgi_ref, dgq_ref, dgk_ref):
             ref[...] = jnp.zeros_like(ref)
 
-    ring_step(2 * step)
+    ring_a(2 * step)
+    ring_b(2 * step)
 
     def attend(c):
         g_q = gain(g_q_ref)
@@ -452,7 +485,12 @@
     def _():
         attend(0)
 
-    ring_step(2 * step + 1)
+    ring_a(2 * step + 1)
+    ring_b(2 * step + 1)
+
+    @pl.when(step > 0)
+    def _():
+        halo(step - 1, 1).start()
 
     @pl.when(step < batch)
     def _():
@@ -462,10 +500,11 @@
 
         @pl.when(step >= 2)
         def _():
-            halo(step - 2).wait_send()
+            for part in range(2):
+                halo(step - 2, part).wait_send()
         halo_out[slot] = ext[:window].astype(BF16)
         dkv_s[slot] = ext[window:]
-        halo(step).start()
+        halo(step, 0).start()
 
     @pl.when(step > 0)
     def _():
@@ -473,8 +512,9 @@
         n, r = unit(x_ref[0].astype(F32))
         g_ai = gain(g_ai_ref)
         h = (n * g_ai).astype(BF16)
-        kn, k_r = unit(dot(h, wqkv_ref[:, q_dim:q_dim + head]))
-        halo(step - 1).wait_recv()
+        kn, k_r = unit(dot(h, wk_ref[...]))
+        for part in range(2):
+            halo(step - 1, part).wait_recv()
         total = dkv_s[slot] + halo_in[step - 1].astype(F32)
         d_kn = rope_back(total[:, :head], cosp_ref[0], sinp_ref[0])
         dgk_ref[...] += colsum(d_kn * kn)
@@ -482,14 +522,16 @@
         d_s[slot, :, q_dim + head:] = total[:, head:].astype(BF16)
         d_all = d_s[slot]
         dw_ref[...] += dot(jnp.transpose(h), d_all)
-        d_h = dot_nt(d_all, wqkv_ref[...])
+        d_h = (dot_nt(d_all[:, :q_dim], wq_ref[...]) + dot_nt(d_all[:, q_dim:q_dim + head], wk_ref[...])
+               + dot_nt(d_all[:, q_dim + head:], wv_ref[...]))
         dgi_ref[...] += colsum(d_h * n)
         dx_ref[0] = (dmid_ref[0] + unit_back(n, r, d_h * g_ai)).astype(BF16)
 
     @pl.when(step == batch)
     def _():
-        halo(batch - 2).wait_send()
-        halo(batch - 1).wait_send()
+        for i in (batch - 2, batch - 1):
+            for part in range(2):
+                halo(i, part).wait_send()
 
 
 def per_seq(shape, lag=None, **kw):
@@ -544,21 +586,20 @@
         inv_freq = ROPE_BASE ** (-2.0 * jnp.arange(half, dtype=F32) / head)
         angles = positions.astype(F32)[..., None] * inv_freq
         cos, sin = jnp.cos(angles), jnp.sin(angles)
-        row = lambda g: g.reshape(1, -1)
-        w_kv = jnp.concatenate([w_key, w_value], axis=1)
-        w_qkv = jnp.concatenate([w_query, w_kv], axis=1)
-        g_ai, g_ao, g_mi, g_mo, g_q, g_k = map(row, (g_attn_in, g_attn_out, g_mlp_in, g_mlp_out, g_query, g_key))
+        top = max(dim, head)
+        g_all = jnp.stack([jnp.pad(g.astype(F32), (0, top - g.shape[0]))
+                           for g in (g_attn_in, g_attn_out, g_mlp_in, g_mlp_out, g_query, g_key)])
         pos_prev = lax.ppermute(positions, "cp", to_next)
         pos_prev = jnp.where(shard_idx > 0, pos_prev, -(2 ** 30))
         pos_ext = jnp.concatenate([pos_prev, positions], axis=1)[:, None, :]
         cs = per_seq(cos.shape)
 
-        (kv,) = call(kv_kernel, n_batch, [x, cos, sin, w_kv, g_ai, g_k],
-                     [per_seq(x.shape), cs, cs, whole(w_kv.shape), whole(g_ai.shape), whole(g_k.shape)],
+        (kv,) = call(kv_kernel, n_batch, [x, cos, sin, w_key, w_value, g_all],
+                     [per_seq(x.shape), cs, cs, whole(w_key.shape), whole(w_value.shape), whole(g_all.shape)],
                      [sds((n_batch, tokens, kv_dim), BF16)], [per_seq((n_batch, tokens, kv_dim))], [], 2 * n_tok * dim * kv_dim)
 
         stack = (n_batch, chunks, heads * qc, head)
-        weights = [w_query, w_out, w_gate, w_up, w_down, g_ai, g_ao, g_mi, g_mo, g_q]
+        weights = [w_query, w_out, w_gate, w_up, w_down, g_all]
         lse_shape = (n_batch, chunks, 1, heads * qc)
         xs = per_seq(x.shape)
         y, d_mid, q_st, qp_st, da_st, lse, big, kv_prev, dg_main = call(
@@ -577,26 +618,27 @@
             collective_id=0, has_side_effects=True)
 
         big = big.reshape(2, chips, slab, wide)
-        part = (slab, wide // 2)
+        part = (slab, max(piece_widths(wide)))
         first, behind = (lambda a: per_seq(a.shape, 0)), (lambda a: per_seq(a.shape, 1))
         seq_in = [kv, kv_prev, cos, sin, pos_ext, q_st, qp_st, da_st, lse]
         lag_in = [x, d_mid, cos, sin]
-        back_w = [w_qkv, g_ai, g_q, g_k]
+        back_w = [w_query, w_key, w_value, g_all]
+        dw_shape = (dim, q_dim + kv_dim)
         dx, dw, dgi, dgq, dgk, full, _ = call(
             functools.partial(back_kernel, window, scale, n_batch), n_batch + 1,
             seq_in + lag_in + [big] + back_w,
             [first(a) for a in seq_in] + [behind(a) for a in lag_in] + [ANY] + [whole(w.shape) for w in back_w],
-            [sds(x.shape, BF16), sds(w_qkv.shape, F32), sds((1, dim), F32), sds((1, head), F32), sds((1, head), F32),
+            [sds(x.shape, BF16), sds(dw_shape, F32), sds((1, dim), F32), sds((1, head), F32), sds((1, head), F32),
              sds(big.shape, BF16), sds(big.shape[1:], F32)],
-            [behind(x), whole(w_qkv.shape), whole((1, dim)), whole((1, head)), whole((1, head)), ANY, ANY],
+            [behind(x), whole(dw_shape), whole((1, dim)), whole((1, head)), whole((1, head)), ANY, ANY],
             [pltpu.VMEM((keys, heads * qc), BF16)] * 2
             + [pltpu.VMEM((window + tokens, kv_dim), F32), pltpu.VMEM((2, tokens, q_dim + kv_dim), BF16),
                pltpu.VMEM((2, tokens, kv_dim), F32), pltpu.VMEM((2, window, kv_dim), BF16),
-               pltpu.VMEM((n_batch, window, kv_dim), BF16), dma((2,)), dma((n_batch,)),
-               pltpu.VMEM((2, 2, 2) + part, F32), pltpu.VMEM((2, 2) + part, BF16),
+               pltpu.VMEM((n_batch, window, kv_dim), BF16), dma((2, 2)), dma((n_batch, 2))]
+            + [pltpu.VMEM((2, 2, 2) + part, F32), pltpu.VMEM((2, 2) + part, BF16),
                pltpu.VMEM((2, chips - 1) + part, BF16), pltpu.VMEM((2,) + part, BF16),
                dma((2, chips)), dma((2, chips)), dma((2, 2, 2)), dma((2, chips - 1)), dma((2, chips - 1)),
-               dma((2, chips - 1)), dma((2, chips - 1)), dma((2, chips)), dma((2, chips)), dma((2,))],
+               dma((2, chips - 1)), dma((2, chips - 1)), dma((2, chips)), dma((2, chips)), dma((2,))] * 2,
             2 * n_tok * (2 * dim * (q_dim + kv_dim) + 5 * q_dim * keys),
             collective_id=1, has_side_effects=True)
 

time: 560 us -> 541 us (0.966)
  Pallas kernels: 439 us -> 428 us
    pallas_call x3, Pallas kernels: 439 us -> 428 us  [call(): pl.pallas_call(kernel, grid=(steps,), in_specs=in_specs, out_specs=out_sp...]
    reshape x6 -> x0, local copies, waits for them, and re-layouts: 6.12 us -> none  [local_step(): row = lambda g: g.reshape(1, -1)]
    unnamed x22 -> x18, local copies, waits for them, and re-layouts: 13 us -> 13 us
  transfers between devices with their start and end apart: 1 -> 1, of which waited for: 0 -> 0; matrix products, arithmetic and copies ran while one was open for 4% -> 3% of each run, Pallas kernels for 2% -> 2%
where the time goes in v2:
time: 541 us; the launch traced here: 540 us
  Pallas kernels  428 us (79%)
  blocking collectives  68.7 us (13%)
  local copies, waits for them, and re-layouts  31 us (6%)
  other arithmetic  10.1 us (2%)
    pallas_call x3, Pallas kernels, call(): pl.pallas_call(kernel, grid=(steps,), in_specs=in_specs, out_specs=out_sp...  428 us
    psum x1, blocking collectives, local_step(): lax.psum((dw, dg_main, dgq, dgi, dgk), 'cp')  68.7 us
    unnamed x18, local copies, waits for them, and re-layouts  13 us
  transfers between devices with their start and end apart: 1, of which 0 were waited for; matrix products, arithmetic and copies ran while one was open for 3% of the time, Pallas kernels for 2%

profile of v2, /device:TPU:30, one launch (start us, length us, event | category | flops | bytes accessed | tf_op | source)
XLA Modules:
  0.0 540.1 jit_solution(12269069225205838952)
XLA Ops:
  0.6 1.8 collective-permute-start
  2.5 0.7 convert_element_type.45
  3.2 0.7 pad.9
  3.9 0.7 pad.10
  4.6 0.7 stack.29
  5.3 0.7 stack.30
  5.9 0.7 stack.31
  6.6 0.7 stack.32
  7.3 0.6 stack.36.g_ref
  8.0 8.8 %multiply_sine_fusion = (f32[8,512,128]{2,1,0:T(8,128)}, f32[8,512,128]{2,1,0:T(8,128)}) fusion(f32[128]{0:T(128)S(1)} %multiply_power_fusion, f32[8,512]{1,0:T(8,128)S(1)} %convert_element_type.45), kind=kLoop, calls=%fused_computation | loop fusion | flops 524288 | bytes 4211200 | tf_op jit(solution)/shard_map/sin | solution.py:588
  16.8 10.7 %shard_map.271.kv_ref.kv_all = bf16[8,512,512]{2,1,0:T(8,128)(2,1)} custom-call(bf16[8,512,640]{2,1,0:T(8,128)(2,1)} %x_ref.5, f32[8,512,128]{2,1,0:T(8,128)} %get-tuple-element.74.cos_ref.cosp_ref, f32[8,512,128]{2,1,0:T(8,128)} %get-tuple-element.73.sin_ref.sinp_ref, bf16[640,256]{1,0:T(8,128)(2,1)} %wk_ref.3, bf16[640,256]{1,0:T(8,128)(2,1)} %wv_ref.3, ...), custom_call_target="tpu_custom_call" | custom-call | flops 2684354560 | bytes 14302208 | tf_op jit(solution)/shard_map/pallas_call | solution.py:554
  27.4 0.0 collective-permute-done
  27.4 0.0 copy-done
  27.4 0.6 broadcast_in_dim.10.pos_ref
  28.1 257.0 %shard_map.272 = (bf16[8,512,640]{2,1,0:T(8,128)(2,1)}, f32[8,512,640]{2,1,0:T(8,128)}, bf16[8,2,1024,256]{3,2,1,0:T(8,128)(2,1)}, f32[8,2,1024,256]{3,2,1,0:T(8...) custom-call(bf16[8,512,640]{2,1,0:T(8,128)(2,1)} %x_ref.5, ...), custom_call_target="tpu_custom_call" | custom-call | flops 130996502528 | bytes 105516032 | tf_op jit(solution)/shard_map/pallas_call | solution.py:554
  285.1 159.9 %shard_map.273 = (bf16[8,512,640]{2,1,0:T(8,128)(2,1)}, f32[640,1536]{1,0:T(8,128)}, f32[1,640]{1,0:T(1,128)}, f32[1,256]{1,0:T(1,128)}, f32[1,256]{1,0:T(1,128)...) custom-call(bf16[8,512,512]{2,1,0:T(8,128)(2,1)} %shard_map.271.kv_ref.kv_all, ...), custom_call_target="tpu_custom_call" | custom-call | flops 48318382080 | bytes 114019840 | tf_op jit(solution)/shard_map/pallas_call | solution.py:554
  445.0 2.5 slice_bitcast_fusion
  447.5 5.3 fusion
  452.8 0.0 copy-done.1
  452.8 0.0 copy-done.2
  452.8 0.0 copy-done.3
  452.8 0.0 copy-done.4
  452.8 68.7 %all-reduce.4 = (bf16[640,1536]{1,0:T(8,128)(2,1)}, bf16[1,640]{1,0:T(2,128)(2,1)S(1)}, bf16[8,640]{1,0:T(8,128)(2,1)S(1)}, bf16[1,256]{1,0:T(2,128)(2,1)S(1)}, bf16[1,256]{1,0:T(2,128)(2,1)S(1)}) all-reduce(f32[640,1536]{1,0:T(8,128)} %get-tuple-element.39, f32[1,640]{1,0:T(1,128)S(1)} %copy-done.2, ...), channel_id=1, replica_groups=mesh['dp'=4,'cp'=16] {'cp'}, use_global_device_ids=true, to_apply=%region_0.1 | all-reduce | flops 989312 | bytes 5935872 | tf_op jit(solution)/shard_map/psum | solution.py:646
  521.5 2.0 fusion.1
  523.5 2.5 slice.46
  525.9 2.6 copy.33
  528.5 2.5 copy.32
  531.0 0.6 slice_reduce_fusion
  531.6 0.5 convert_reduce_fusion.1
  532.2 5.5 %copy.46 = bf16[8,512,640]{2,1,0:T(8,128)(2,1)} copy(bf16[8,512,640]{2,1,0:T(8,128)(2,1)} %get-tuple-element.93) | data formatting | bytes 10485760
  537.7 0.0 slice-done
  537.7 2.4 copy.47
  (15 shorter events, 0.1 us)
Async XLA Ops:
  0.6 26.8 %collective-permute-start = (s32[8,512]{1,0:T(8,128)}, s32[8,512]{1,0:T(8,128)S(1)}, u32[]{:S(2)}, u32[]{:S(2)}) collective-permute-start(s32[8,512]{1,0:T(8,128)} %param.18), channel_id=1, source_target_pairs={{0,1},{1,2},{2,3},{3,4},{4,5},{5,6},{6,7},{7,8},{8,9},{9,10},{10,1... | collective-permute-start | bytes 49160 | tf_op jit(solution)/shard_map/ppermute | solution.py:592
  16.8 10.7 %copy-start = (s32[8,512]{1,0:T(8,128)S(1)}, s32[8,512]{1,0:T(8,128)}, u32[]{:S(2)}) copy-start(s32[8,512]{1,0:T(8,128)} %param.18) | copy-start | bytes 49156
  447.5 5.3 copy-start.1
  447.5 5.3 copy-start.2
  447.5 5.3 copy-start.3
  447.5 5.3 copy-start.4
  528.5 9.2 %slice-start = ((s8[5242880]{0:T(1024)(128)(4,1)}), s8[1048576]{0:T(1024)(128)(4,1)S(1)}, s32[]{:S(2)}) async-start(s8[5242880]{0:T(1024)(128)(4,1)} %bitcast.7), calls=%async_computation | async-start | bytes 2097152
  532.2 5.6 %slice-start.1 = ((s8[5242880]{0:T(1024)(128)(4,1)}), s8[4194304]{0:T(1024)(128)(4,1)S(1)}, s32[]{:S(2)}) async-start(s8[5242880]{0:T(1024)(128)(4,1)} %bitcast.7), calls=%async_computation.1 | async-start | bytes 8388608
